TPU v7x, 32 devices: a whole 2x2x4 slice. The times are simulated.
32 devices in a mesh: samp: 16 (over z, y, core), var: 2 (over x).
Axes of the slice: x: 2, y: 2, z: 4, core: 2. Of those that a mesh axis runs over, the one named last changes fastest.
Arguments:
- dosages: bfloat16 [8192, 3584], P('samp', 'var'), may hold values from 0 to 2
- weights: bfloat16 [3584, 512], P('var'), may hold values from -0.09375 to 0.09375
- prior: float32 [8192, 512], P('samp', 'var'), may hold values from -6 to 6
- cohort: int32 [8192, 1], P('samp'), may hold values from 0 to 15
- expression: bfloat16 [8192, 10240], P('samp', 'var'), may hold values from -6 to 6
Outputs:
- correlation: float32 [512, 10240], P('samp', 'var')
Inputs may be any that keep to these rules, and one draw needn't show every extreme that they name: Every cohort has at least one sample.
All inputs are finite; a program needn't handle non-finite values.
Results may differ from a plain program's by a relative error of at most 0.0042.
Values may be sent and summed in bfloat16 or wider, within the bound.
No kernel may reach another device: no remote copies, remote signals or barrier semaphores. Data moves between devices by JAX's collectives and lax.ppermute only.
A program may use at most 64 MiB of HBM per device.

v0:
```python
import jax
import jax.numpy as jnp
from jax import lax
from jax.sharding import PartitionSpec as P

COHORTS = 16


def standardize(scores, onehot):
    sums = jnp.dot(onehot.T, scores, precision=lax.Precision.HIGHEST)
    counts = jnp.sum(onehot, axis=0)
    raw_squares = jnp.sum(scores * scores, axis=0)
    sums, counts, raw_squares = lax.psum((sums, counts, raw_squares), "samp")
    means = sums / counts[:, None]
    centered = scores - jnp.dot(onehot, means, precision=lax.Precision.HIGHEST)
    squares = raw_squares - jnp.sum(sums * means, axis=0)
    total = jnp.sum(counts)
    spread = lax.rsqrt(squares / total + 1e-06)
    return ((centered * spread[None, :]).astype(jnp.bfloat16), total)


def shards(dosages, weights, prior, cohort, expression):
    width = prior.shape[1]
    offset = lax.axis_index("var") * width
    partial_value = jnp.dot(dosages, weights, preferred_element_type=jnp.float32)
    own_part = lax.dynamic_slice_in_dim(partial_value, offset, width, 1) + prior
    partial_value = lax.dynamic_update_slice_in_dim(partial_value, own_part, offset, 1)
    onehot = (cohort == jnp.arange(COHORTS, dtype=jnp.int32)[None, :]).astype(jnp.float32)
    scores = lax.psum(partial_value, "var")
    standard, total = standardize(scores, onehot)
    cross = lax.psum_scatter(
        lax.dot_general(
            standard, expression, (((0,), (0,)), ((), ())), preferred_element_type=jnp.float32
        ),
        "samp",
        scatter_dimension=0,
        tiled=True,
    )
    return cross / total


def solution(mesh):
    placed = (P("samp", "var"), P("var", None), P("samp", "var"), P("samp", None), P("samp", "var"))
    return jax.shard_map(
        shards, mesh=mesh, in_specs=placed, out_specs=P("samp", "var"), check_vma=False
    )
```

profile of v0, /device:TPU:0, one launch (start us, length us, event | category | flops | bytes accessed | tf_op | source)
XLA Modules:
  0.0 254.6 jit_solution(17596841640820288969)
XLA Ops:
  6.5 0.0 copy-start
  6.5 0.0 all-reduce.3.cloned.1.call-start
  6.5 1.5 copy-done
  8.0 0.0 copy-start.3
  8.0 2.7 %fusion.7 = f32[512,512]{1,0:T(8,128)S(1)} fusion(bf16[512,1792]{1,0:T(8,128)(2,1)S(1)} %copy-done, bf16[1792,512]{1,0:T(8,128)(2,1)} %param.6), kind=kOutput, calls=%fused_computation.15 | convolution fusion | flops 939524096 | bytes 4718592 | tf_op jit(solution)/shard_map/dot_general | solution.py:25
  10.7 0.0 copy-done.3
  10.7 0.0 copy-start.4
  10.7 0.1 add_dynamic-update-slice_fusion
  10.9 0.0 copy-start.2
  10.9 1.0 copy-done.2
  11.9 0.0 all-reduce.3.cloned.1.call-update
  11.9 0.0 reduce-scatter.2.cloned.1.call-start
  12.0 0.0 copy-done.4
  12.0 0.1 convert_reduce_fusion
  12.1 42.8 %all-reduce.3.cloned.1.call-done = f32[512,512]{1,0:T(8,128)} async-done(((f32[512,512]{1,0:T(8,128)}), f32[512,512]{1,0:T(8,128)}) %all-reduce.3.cloned.1.call-update) | async-done | bytes 1048592 | tf_op jit(solution)/shard_map/psum | solution.py:29
  54.9 0.0 copy-start.1
  54.9 1.4 multiply_reduce_fusion
  56.3 1.7 fusion.2
  58.0 61.0 %all-reduce = (f32[512]{0:T(512)S(1)}, f32[16,512]{1,0:T(8,128)S(1)}, f32[16]{0:T(128)S(1)}) all-reduce(f32[512]{0:T(512)S(1)} %multiply_reduce_fusion, f32[16,512]{1,0:T(8,128)S(1)} %fusion.2, f32[16]{0:T(128)S(1)} %convert_reduce_fusion), channel_id=1, replica_groups=mesh['samp'=16,'var'=2] {'samp'}, use_global_device_ids=true, to_apply=%region_5.0 | all-reduce | flops 8720 | bytes 69760 | tf_op jit(solution)/shard_map/psum | solution.py:13
  119.0 0.6 reduce_sum.39
  119.7 0.1 multiply_reduce_fusion.1
  119.8 0.6 add_rsqrt_fusion
  120.4 0.0 copy-done.1
  120.4 0.7 fusion.1
  121.1 8.1 %fusion.8 = f32[512,5120]{1,0:T(8,128)} fusion(bf16[512,512]{1,0:T(8,128)(2,1)S(1)} %fusion.1, bf16[512,5120]{1,0:T(8,128)(2,1)} %param.9), kind=kOutput, calls=%fused_computation.16 | convolution fusion | flops 2684354560 | bytes 16252928 | tf_op jit(solution)/shard_map/dot_general | solution.py:32
  129.1 0.0 reduce-scatter.2.cloned.1.call-update
  129.1 116.0 %reduce-scatter.2.cloned.1.call-done = f32[32,5120]{1,0:T(8,128)} async-done(((f32[512,5120]{1,0:T(8,128)}), f32[32,5120]{1,0:T(8,128)}) %reduce-scatter.2.cloned.1.call-update) | async-done | bytes 655376 | tf_op jit(solution)/shard_map/reduce_scatter | solution.py:31
  245.1 2.6 %broadcast_divide_fusion = f32[32,5120]{1,0:T(8,128)} fusion(f32[32,5120]{1,0:T(8,128)} %reduce-scatter.2.cloned.1.call-done, f32[]{:T(128)} %reduce_sum.39), kind=kLoop, calls=%fused_computation.5 | loop fusion | flops 163840 | bytes 1310724 | tf_op jit(solution)/shard_map/div | solution.py:39
Async XLA Ops:
  6.5 1.5 copy-start
  6.5 48.4 %all-reduce.3.cloned.1.call-start = ((), (), s32[]{:S(2)}) async-start(), calls=%async_computation.1 | async-start | bytes 2097152 | tf_op jit(solution)/shard_map/psum | solution.py:29
  8.0 2.7 %copy-start.3 = (f32[512,256]{1,0:T(8,128)S(1)}, f32[512,256]{1,0:T(8,128)}, u32[]{:S(2)}) copy-start(f32[512,256]{1,0:T(8,128)} %param.7) | copy-start | bytes 1572868
  10.7 1.3 copy-start.4
  10.9 1.0 copy-start.2
  11.9 233.2 %reduce-scatter.2.cloned.1.call-start = ((), (), s32[]{:S(2)}) async-start(), calls=%async_computation.2 | async-start | bytes 11141120 | tf_op jit(solution)/shard_map/reduce_scatter | solution.py:31
  54.9 65.5 %copy-start.1 = (f32[512,512]{1,0:T(8,128)S(1)}, f32[512,512]{1,0:T(8,128)}, u32[]{:S(2)}) copy-start(f32[512,512]{1,0:T(8,128)} %all-reduce.3.cloned.1.call-done) | copy-start | bytes 3145732
Sparse Core Ops, SparseCore 0:
  12.0 42.8 all-reduce.2
  129.3 115.8 reduce-scatter.1
where the time goes:
time: 255 us
  waiting for transfers between devices  159 us (62%)
  blocking collectives  61 us (24%)
  between operations  13.5 us (5%)
  matrix products  13.1 us (5%)
  other arithmetic  5.58 us (2%)
    reduce_scatter x1, waiting for transfers between devices, shards(): lax.psum_scatter(lax.dot_general(standard, expression, (((0,), (0,)), (()...  116 us
    psum x1, blocking collectives, standardize(): sums, counts, raw_squares = lax.psum((sums, counts, raw_squares), 'samp')  61 us
    psum x1, waiting for transfers between devices, shards(): scores = lax.psum(partial_value, 'var')  42.8 us
    dot_general x1, matrix products, shards(): lax.dot_general(standard, expression, (((0,), (0,)), ((), ())), preferred...  8.05 us
  transfers between devices with their start and end apart: 2, of which 2 were waited for; matrix products, arithmetic and copies ran while one was open for 0% of the time, Pallas kernels for 0%

commit v1 on v0

v1 whole, which is shorter than its diff:
```python
import jax
import jax.numpy as jnp
from jax import lax
from jax.sharding import PartitionSpec as P

COHORTS = 16
GENE_CHUNKS = 2
BF16, F32 = jnp.bfloat16, jnp.float32
EXACT = lax.Precision.HIGHEST


def flip(size, stride):
    return [(i, i ^ stride) for i in range(size)]


def shift(size, step):
    return [(i, (i + step) % size) for i in range(size)]


def strides(size):
    return [1 << bit for bit in range(size.bit_length() - 1)]


def pick(array, index, axis):
    return lax.dynamic_index_in_dim(array, index, axis, keepdims=False)


def all_sum(value, size):
    for stride in strides(size):
        value = value + lax.ppermute(value, "samp", flip(size, stride))
    return value


def scatter_sum(standard, expression, place, size):
    owners, rows, samples = standard.shape

    def product(lhs):
        return lax.dot_general(
            lhs, expression, (((2,), (0,)), ((), ())), preferred_element_type=F32
        )

    halves = standard.reshape(owners // 2, 2, rows, samples)
    bit = place & 1
    sent = product(pick(halves, 1 - bit, 1)).astype(BF16)
    total = product(pick(halves, bit, 1)) + lax.ppermute(sent, "samp", flip(size, 1)).astype(F32)
    for stride in strides(size)[1:]:
        bit = (place // stride) & 1
        halves = total.reshape(total.shape[0] // 2, 2, rows, -1)
        sent = pick(halves, 1 - bit, 1).astype(BF16)
        total = pick(halves, bit, 1) + lax.ppermute(sent, "samp", flip(size, stride)).astype(F32)
    return total[0]


def shards(dosages, weights, prior, cohort, expression, *, size, parts):
    place, part = lax.axis_index("samp"), lax.axis_index("var")
    samples, width = prior.shape
    rows = width // size
    genes = expression.shape[1]

    scores = lax.dot_general(
        weights, dosages, (((0,), (1,)), ((), ())), preferred_element_type=F32
    ).reshape(size, parts, rows, samples)
    at = part * (size // parts)
    own = lax.dynamic_slice_in_dim(scores, at, size // parts, 0)
    own = own + prior.T.reshape(size // parts, parts, rows, samples)
    scores = lax.dynamic_update_slice_in_dim(scores, own, at, 0)

    member = cohort[:, 0][None, :] == jnp.arange(COHORTS, dtype=jnp.int32)[:, None]
    member = member.astype(F32)
    counts = jnp.sum(member, axis=1)

    def cohort_sums(values):
        return lax.dot_general(
            member, values.reshape(size * rows, samples), (((1,), (1,)), ((), ())), precision=EXACT
        )

    scored = pick(scores, part, 1)
    sums = cohort_sums(scored)
    for step in range(1, parts):
        values = pick(scores, (part + step) % parts, 1)
        offset = jnp.mean(values, axis=2, keepdims=True)
        small = jnp.concatenate([cohort_sums(values), offset.reshape(1, -1)], axis=0)
        small = lax.ppermute(small, "var", shift(parts, step))
        sums = sums + small[:COHORTS]
        values = lax.ppermute((values - offset).astype(BF16), "var", shift(parts, step))
        scored = scored + values.astype(F32) + small[COHORTS].reshape(size, rows, 1)
    small = jnp.concatenate(
        [sums, jnp.broadcast_to(counts[:, None], (COHORTS, 128))], axis=1
    )
    small = all_sum(small, size)
    sums, counts = small[:, :-128], small[:, -1]
    means = sums / counts[:, None]
    total = jnp.sum(counts)
    centered = scored - lax.dot_general(
        means, member, (((0,), (0,)), ((), ())), precision=EXACT
    ).reshape(scored.shape)

    standard = [centered.astype(BF16)]
    squares = [jnp.sum(centered * centered, axis=2)]
    for step in range(1, parts):
        standard.append(lax.ppermute(standard[0], "var", shift(parts, step)))
        wide = standard[step].astype(F32)
        squares.append(jnp.sum(wide * wide, axis=2))
    chunk = genes // GENE_CHUNKS
    sums = [
        [
            scatter_sum(values, expression[:, at : at + chunk], place, size)
            for at in range(0, genes, chunk)
        ]
        for values in standard
    ]
    squares = all_sum(jnp.stack(squares), size)
    spread = pick(lax.rsqrt(squares / total + 1e-06) / total, place, 1)
    result = jnp.zeros((parts, rows, genes), F32)
    for step in range(parts):
        values = jnp.concatenate(sums[step], axis=1) * spread[step][:, None]
        result = lax.dynamic_update_slice_in_dim(
            result, values[None], (part - step) % parts, 0
        )
    return result.reshape(parts * rows, genes)


def solution(mesh):
    size, parts = mesh.shape["samp"], mesh.shape["var"]

    def step(*arrays):
        return shards(*arrays, size=size, parts=parts)

    placed = (P("samp", "var"), P("var", None), P("samp", "var"), P("samp", None), P("samp", "var"))
    return jax.shard_map(
        step, mesh=mesh, in_specs=placed, out_specs=P("samp", "var"), check_vma=False
    )
```

time: 255 us -> 103 us (0.40)
  waiting for transfers between devices: 159 us -> 36.9 us
  blocking collectives: 61 us -> 0 us
  starting transfers between devices: 0.04 us -> 39.8 us
  between operations: 13.5 us -> 0.41 us
  other arithmetic: 5.58 us -> 8.5 us
    reduce_scatter x1 -> x0, waiting for transfers between devices: 116 us -> none  [shards(): lax.psum_scatter(lax.dot_general(standard, expression, (((0,), (0,)), (()...]
    psum x1 -> x0, blocking collectives: 61 us -> none  [standardize(): sums, counts, raw_squares = lax.psum((sums, counts, raw_squares), 'samp')]
    psum x1 -> x0, waiting for transfers between devices: 42.8 us -> none  [shards(): scores = lax.psum(partial_value, 'var')]
    ppermute x0 -> x27, starting transfers between devices: none -> 39.8 us  [the longest x12 20.1 us: scatter_sum(): lax.ppermute(sent, 'samp', flip(size, stride)).astype(F32)]
    ppermute x0 -> x27, waiting for transfers between devices: none -> 36.9 us  [the longest x12 22.6 us: scatter_sum(): lax.ppermute(sent, 'samp', flip(size, stride)).astype(F32)]
    dot_general x4 -> x12, matrix products: 13.1 us -> 13.6 us  [the longest x8 7.67 us: product(): lax.dot_general(lhs, expression, (((2,), (0,)), ((), ())), preferred_elem...]
  transfers between devices with their start and end apart: 2 -> 27, of which waited for: 2 -> 14; matrix products, arithmetic and copies ran while one was open for 0% -> 11% of each run, Pallas kernels for 0% -> 0%
where the time goes in v1:
time: 103 us; the launch traced here: 102 us
  starting transfers between devices  39.8 us (39%)
  waiting for transfers between devices  36.9 us (36%)
  matrix products  13.6 us (13%)
  other arithmetic  8.5 us (8%)
  local copies, waits for them, and re-layouts  3.15 us (3%)
    ppermute x12, waiting for transfers between devices, scatter_sum(): lax.ppermute(sent, 'samp', flip(size, stride)).astype(F32)  22.6 us
    ppermute x12, starting transfers between devices, scatter_sum(): lax.ppermute(sent, 'samp', flip(size, stride)).astype(F32)  20.1 us
    ppermute x8, starting transfers between devices, all_sum(): value = value + lax.ppermute(value, 'samp', flip(size, stride))  12.6 us
    dot_general x8, matrix products, product(): lax.dot_general(lhs, expression, (((2,), (0,)), ((), ())), preferred_elem...  7.67 us
    ppermute x8, waiting for transfers between devices, all_sum(): value = value + lax.ppermute(value, 'samp', flip(size, stride))  7.65 us
    ppermute x1, waiting for transfers between devices, shards(): standard.append(lax.ppermute(standard[0], 'var', shift(parts, step)))  4.98 us
    dot_general x1, matrix products, shards(): lax.dot_general(weights, dosages, (((0,), (1,)), ((), ())), preferred_ele...  3.65 us
    ppermute x1, starting transfers between devices, shards(): small = lax.ppermute(small, 'var', shift(parts, step))  3.05 us
  transfers between devices with their start and end apart: 27, of which 14 were waited for; matrix products, arithmetic and copies ran while one was open for 11% of the time, Pallas kernels for 0%

profile of v1, /device:TPU:0, one launch (start us, length us, event | category | flops | bytes accessed | tf_op | source)
XLA Modules:
  0.0 102.4 jit_solution(16434513676246208775)
XLA Ops:
  0.0 1.4 %copy.24 = f32[512,256]{0,1:T(8,128)S(1)} copy(f32[512,256]{1,0:T(8,128)} %param.7) | data formatting | bytes 1048576 | tf_op args[2]
  1.7 3.6 %fusion.76 = f32[512,512]{1,0:T(8,128)} fusion(bf16[1792,512]{1,0:T(8,128)(2,1)S(1)} %copy-done, bf16[512,1792]{1,0:T(8,128)(2,1)} %param.5), kind=kOutput, calls=%fused_computation.125 | convolution fusion | flops 939524096 | bytes 4718592 | tf_op jit(solution)/shard_map/dot_general | solution.py:60
  5.3 1.9 %add_dynamic-update-slice_fusion = f32[16,2,16,512]{3,2,1,0:T(8,128)} fusion(f32[16,2,16,512]{3,2,1,0:T(8,128)} %bitcast, s32[]{:T(128)S(6)} %select_n.107, f32[8,2,16,512]{3,2,1,0:T(8,128)S(1)} %bitcast.159), kind=kLoop, calls=%fused_computation.41 | loop fusion | flops 131072 | bytes 1572868 | tf_op jit(solution)/shard_map/dynamic_update_slice | solution.py:66
  7.2 2.2 %fusion.75 = (f32[16,16]{1,0:T(8,128)S(1)}, f32[16,1,16,512]{3,2,1,0:T(8,128)S(1)}, f32[16,1,16,512]{3,2,1,0:T(8,128)}) fusion(f32[16,2,16,512]{3,2,1,0:T(8,128)} %add_dynamic-update-slice_fusion, s32[]{:T(128)S(6)} %select_n.110, s32[]{:T(128)S(6)} %select_n.108), kind=kLoop, calls=%fused_computation.124 | loop fusion | flops 130816 | bytes 2098184 | tf_op jit(solution)/shard_map/reduce_sum | solution.py:81
  9.9 3.0 %collective-permute-start.1 = (f32[17,256]{1,0:T(8,128)S(1)}, f32[17,256]{1,0:T(8,128)S(1)}, u32[]{:S(2)}, u32[]{:S(2)}) collective-permute-start(f32[17,256]{1,0:T(8,128)S(1)} %pad_maximum_fusion), channel_id=1, source_target_pairs={{0,1},{1,0},{2,3},{3,2},{4,5},{5,4},{6,7},{7,6},{8,9},{9,8},{10,11... | collective-permute-start | bytes 52232 | tf_op jit(solution)/shard_map/ppermute | solution.py:83
  13.0 1.7 %collective-permute-done.1 = f32[17,256]{1,0:T(8,128)S(1)} collective-permute-done((f32[17,256]{1,0:T(8,128)S(1)}, f32[17,256]{1,0:T(8,128)S(1)}, u32[]{:S(2)}, u32[]{:S(2)}) %collective-permute-start.1) | collective-permute-done | bytes 17440 | tf_op jit(solution)/shard_map/ppermute | solution.py:83
  14.7 1.4 %slice_add_fusion = f32[16,256]{1,0:T(8,128)S(1)} fusion(f32[17,256]{1,0:T(8,128)S(1)} %collective-permute-done.1, f32[256,512]{1,0:T(8,128)} %bitcast.149, s32[512]{0:T(512)S(1)} %bitcast.184), kind=kOutput, calls=%fused_computation.95 | convolution fusion | flops 25178112 | bytes 559104 | tf_op jit(solution)/shard_map/dot_general | solution.py:73
  16.2 1.2 %collective-permute-done.2 = f32[16,384]{1,0:T(8,128)S(1)} collective-permute-done((f32[16,384]{1,0:T(8,128)S(1)}, f32[16,384]{1,0:T(8,128)S(1)}, u32[]{:S(2)}, u32[]{:S(2)}) %collective-permute-start.2) | collective-permute-done | bytes 24608 | tf_op jit(solution)/shard_map/ppermute | solution.py:30
  17.4 2.0 %collective-permute-start.3 = (f32[16,384]{1,0:T(8,128)S(1)}, f32[16,384]{1,0:T(8,128)S(1)}, u32[]{:S(2)}, u32[]{:S(2)}) collective-permute-start(f32[16,384]{1,0:T(8,128)S(1)} %fusion.73), channel_id=1, source_target_pairs={{0,4},{2,6},{4,0},{6,2},{8,12},{10,14},{12,8},{14,10},{16,20},{18,... | collective-permute-start | bytes 73736 | tf_op jit(solution)/shard_map/ppermute | solution.py:30
  19.4 1.8 %collective-permute-done.3 = f32[16,384]{1,0:T(8,128)S(1)} collective-permute-done((f32[16,384]{1,0:T(8,128)S(1)}, f32[16,384]{1,0:T(8,128)S(1)}, u32[]{:S(2)}, u32[]{:S(2)}) %collective-permute-start.3) | collective-permute-done | bytes 24608 | tf_op jit(solution)/shard_map/ppermute | solution.py:30
  21.3 2.1 %collective-permute-start.4 = (f32[16,384]{1,0:T(8,128)S(1)}, f32[16,384]{1,0:T(8,128)S(1)}, u32[]{:S(2)}, u32[]{:S(2)}) collective-permute-start(f32[16,384]{1,0:T(8,128)S(1)} %add.203), channel_id=1, source_target_pairs={{0,8},{2,10},{4,12},{6,14},{8,0},{10,2},{12,4},{14,6},{16,24},{18,... | collective-permute-start | bytes 73736 | tf_op jit(solution)/shard_map/ppermute | solution.py:30
  23.3 0.8 fusion.18
  24.1 1.5 %collective-permute-start = (bf16[16,16,512]{2,1,0:T(8,128)(2,1)}, bf16[16,16,512]{2,1,0:T(8,128)(2,1)S(1)}, u32[]{:S(2)}, u32[]{:S(2)}) collective-permute-start(bf16[16,16,512]{2,1,0:T(8,128)(2,1)} %fusion.18), channel_id=1, source_target_pairs={{0,1},{1,0},{2,3},{3,2},{4,5},{5,4},{6,7},{7,6},{8,9},{9,8},{10,11... | collective-permute-start | bytes 786440 | tf_op jit(solution)/shard_map/ppermute | solution.py:85
  25.6 2.7 %collective-permute-start.5 = (f32[16,384]{1,0:T(8,128)S(1)}, f32[16,384]{1,0:T(8,128)S(1)}, u32[]{:S(2)}, u32[]{:S(2)}) collective-permute-start(f32[16,384]{1,0:T(8,128)S(1)} %add.204), channel_id=1, source_target_pairs={{0,16},{2,18},{4,20},{6,22},{8,24},{10,26},{12,28},{14,30},{16,0},... | collective-permute-start | bytes 73736 | tf_op jit(solution)/shard_map/ppermute | solution.py:30
  28.4 2.0 %collective-permute-done.5 = f32[16,384]{1,0:T(8,128)S(1)} collective-permute-done((f32[16,384]{1,0:T(8,128)S(1)}, f32[16,384]{1,0:T(8,128)S(1)}, u32[]{:S(2)}, u32[]{:S(2)}) %collective-permute-start.5) | collective-permute-done | bytes 24608 | tf_op jit(solution)/shard_map/ppermute | solution.py:30
  30.4 0.7 slice_reduce_fusion
  31.7 1.3 %multiply_reduce_fusion.1 = (f32[16,16]{1,0:T(8,128)S(1)}, bf16[16,16,512]{2,1,0:T(8,128)(2,1)S(1)}) fusion(f32[16,16,512]{2,1,0:T(8,128)S(1)} %bitcast.150, f32[16,16]{1,0:T(8,128)S(1)} %add.198, bf16[16,16,512]{2,1,0:T(8,128)(2,1)S(1)} %collective-permute-done, f32[16,1,16,512]{3,2,1,0:T(8,128)} %get-tuple-element.9, f32[256,512]{1,0:T(8,128)S(1)} %fusion.56), kind=kLoop, calls=%fused_computation.40 | loop fusion | flops 1048320 | bytes 2099200 | tf_op jit(solution)/shard_map/reduce_sum | solution.py:99
  33.0 1.5 %collective-permute-start.14 = (bf16[16,16,512]{2,1,0:T(8,128)(2,1)S(1)}, bf16[16,16,512]{2,1,0:T(8,128)(2,1)S(1)}, u32[]{:S(2)}, u32[]{:S(2)}) collective-permute-start(bf16[16,16,512]{2,1,0:T(8,128)(2,1)S(1)} %get-tuple-element.11), channel_id=1, source_target_pairs={{0,1},{1,0},{2,3},{3,2},{4,5},{5,4},{6,7},{7,6},{8,9},{9,8},{10,11... | collective-permute-start | bytes 786440 | tf_op jit(solution)/shard_map/ppermute | solution.py:101
  34.4 5.0 %collective-permute-done.14 = bf16[16,16,512]{2,1,0:T(8,128)(2,1)S(1)} collective-permute-done((bf16[16,16,512]{2,1,0:T(8,128)(2,1)S(1)}, bf16[16,16,512]{2,1,0:T(8,128)(2,1)S(1)}, u32[]{:S(2)}, u32[]{:S(2)}) %collective-permute-start.14) | collective-permute-done | bytes 262176 | tf_op jit(solution)/shard_map/ppermute | solution.py:101
  39.7 2.3 %convolution_convert_fusion.3 = bf16[8,16,2560]{2,1,0:T(8,128)(2,1)S(1)} fusion(bf16[512,5120]{1,0:T(8,128)(2,1)} %param.9, bf16[8,2,16,512]{3,2,1,0:T(8,128)(2,1)S(1)} %bitcast.172, s32[]{:T(128)S(6)} %select_n.112), kind=kOutput, calls=%fused_computation.5 | convolution fusion | flops 335872000 | bytes 3407876 | tf_op jit(solution)/shard_map/dot_general | solution.py:38
  41.9 1.6 %collective-permute-start.16 = (f32[2,16,16]{2,1,0:T(8,128)S(1)}, f32[2,16,16]{2,1,0:T(8,128)S(1)}, u32[]{:S(2)}, u32[]{:S(2)}) collective-permute-start(f32[2,16,16]{2,1,0:T(8,128)S(1)} %fusion.74), channel_id=1, source_target_pairs={{0,4},{2,6},{4,0},{6,2},{8,12},{10,14},{12,8},{14,10},{16,20},{18,... | collective-permute-start | bytes 6152 | tf_op jit(solution)/shard_map/ppermute | solution.py:30
  43.5 2.3 %convolution_convert_fusion.2 = bf16[8,16,2560]{2,1,0:T(8,128)(2,1)S(1)} fusion(bf16[512,5120]{1,0:T(8,128)(2,1)} %param.9, bf16[8,2,16,512]{3,2,1,0:T(8,128)(2,1)S(1)} %bitcast.173, s32[]{:T(128)S(6)} %select_n.112), kind=kOutput, calls=%fused_computation.4 | convolution fusion | flops 335872000 | bytes 3407876 | tf_op jit(solution)/shard_map/dot_general | solution.py:38
  46.4 1.5 %collective-permute-start.17 = (f32[2,16,16]{2,1,0:T(8,128)S(1)}, f32[2,16,16]{2,1,0:T(8,128)S(1)}, u32[]{:S(2)}, u32[]{:S(2)}) collective-permute-start(f32[2,16,16]{2,1,0:T(8,128)S(1)} %fusion.81), channel_id=1, source_target_pairs={{0,8},{2,10},{4,12},{6,14},{8,0},{10,2},{12,4},{14,6},{16,24},{18,... | collective-permute-start | bytes 6152 | tf_op jit(solution)/shard_map/ppermute | solution.py:30
  48.4 1.8 %collective-permute-done.17 = f32[2,16,16]{2,1,0:T(8,128)S(1)} collective-permute-done((f32[2,16,16]{2,1,0:T(8,128)S(1)}, f32[2,16,16]{2,1,0:T(8,128)S(1)}, u32[]{:S(2)}, u32[]{:S(2)}) %collective-permute-start.17) | collective-permute-done | bytes 2080 | tf_op jit(solution)/shard_map/ppermute | solution.py:30
  50.2 2.7 %collective-permute-start.18 = (f32[2,16,16]{2,1,0:T(8,128)S(1)}, f32[2,16,16]{2,1,0:T(8,128)S(1)}, u32[]{:S(2)}, u32[]{:S(2)}) collective-permute-start(f32[2,16,16]{2,1,0:T(8,128)S(1)} %add.224), channel_id=1, source_target_pairs={{0,16},{2,18},{4,20},{6,22},{8,24},{10,26},{12,28},{14,30},{16,0},... | collective-permute-start | bytes 6152 | tf_op jit(solution)/shard_map/ppermute | solution.py:30
  54.0 0.9 collective-permute-done.18
  54.8 0.7 rsqrt_divide_fusion
  55.5 0.5 convert_add_fusion.1
  56.1 0.9 collective-permute-start.7
  57.6 1.3 %collective-permute-start.11 = (bf16[4,16,2560]{2,1,0:T(8,128)(2,1)S(1)}, bf16[4,16,2560]{2,1,0:T(8,128)(2,1)S(1)}, u32[]{:S(2)}, u32[]{:S(2)}) collective-permute-start(bf16[4,16,2560]{2,1,0:T(8,128)(2,1)S(1)} %fusion.22), channel_id=1, source_target_pairs={{0,4},{2,6},{4,0},{6,2},{8,12},{10,14},{12,8},{14,10},{16,20},{18,... | collective-permute-start | bytes 983048 | tf_op jit(solution)/shard_map/ppermute | solution.py:50
  59.4 0.9 collective-permute-start.20
  60.4 0.5 convolution_add_fusion
  60.9 1.3 %collective-permute-start.24 = (bf16[4,16,2560]{2,1,0:T(8,128)(2,1)S(1)}, bf16[4,16,2560]{2,1,0:T(8,128)(2,1)S(1)}, u32[]{:S(2)}, u32[]{:S(2)}) collective-permute-start(bf16[4,16,2560]{2,1,0:T(8,128)(2,1)S(1)} %fusion.24), channel_id=1, source_target_pairs={{0,4},{2,6},{4,0},{6,2},{8,12},{10,14},{12,8},{14,10},{16,20},{18,... | collective-permute-start | bytes 983048 | tf_op jit(solution)/shard_map/ppermute | solution.py:50
  62.2 4.5 %collective-permute-done.7 = bf16[4,16,2560]{2,1,0:T(8,128)(2,1)S(1)} collective-permute-done((bf16[4,16,2560]{2,1,0:T(8,128)(2,1)S(1)}, bf16[4,16,2560]{2,1,0:T(8,128)(2,1)S(1)}, u32[]{:S(2)}, u32[]{:S(2)}) %collective-permute-start.7) | collective-permute-done | bytes 327712 | tf_op jit(solution)/shard_map/ppermute | solution.py:50
  66.8 1.5 %collective-permute-start.8 = (bf16[2,16,2560]{2,1,0:T(8,128)(2,1)S(1)}, bf16[2,16,2560]{2,1,0:T(8,128)(2,1)S(1)}, u32[]{:S(2)}, u32[]{:S(2)}) collective-permute-start(bf16[2,16,2560]{2,1,0:T(8,128)(2,1)S(1)} %fusion.27), channel_id=1, source_target_pairs={{0,8},{2,10},{4,12},{6,14},{8,0},{10,2},{12,4},{14,6},{16,24},{18,... | collective-permute-start | bytes 491528 | tf_op jit(solution)/shard_map/ppermute | solution.py:50
  68.4 5.4 %collective-permute-done.11 = bf16[4,16,2560]{2,1,0:T(8,128)(2,1)S(1)} collective-permute-done((bf16[4,16,2560]{2,1,0:T(8,128)(2,1)S(1)}, bf16[4,16,2560]{2,1,0:T(8,128)(2,1)S(1)}, u32[]{:S(2)}, u32[]{:S(2)}) %collective-permute-start.11) | collective-permute-done | bytes 327712 | tf_op jit(solution)/shard_map/ppermute | solution.py:50
  73.9 1.5 %collective-permute-start.12 = (bf16[2,16,2560]{2,1,0:T(8,128)(2,1)S(1)}, bf16[2,16,2560]{2,1,0:T(8,128)(2,1)S(1)}, u32[]{:S(2)}, u32[]{:S(2)}) collective-permute-start(bf16[2,16,2560]{2,1,0:T(8,128)(2,1)S(1)} %fusion.28), channel_id=1, source_target_pairs={{0,8},{2,10},{4,12},{6,14},{8,0},{10,2},{12,4},{14,6},{16,24},{18,... | collective-permute-start | bytes 491528 | tf_op jit(solution)/shard_map/ppermute | solution.py:50
  75.5 2.9 %collective-permute-start.9 = (bf16[1,16,2560]{2,1,0:T(8,128)(2,1)S(1)}, bf16[1,16,2560]{2,1,0:T(8,128)(2,1)S(1)}, u32[]{:S(2)}, u32[]{:S(2)}) collective-permute-start(bf16[1,16,2560]{2,1,0:T(8,128)(2,1)S(1)} %dynamic-slice_convert_fusion.7), channel_id=1, source_target_pairs={{0,16},{2,18},{4,20},{6,22},{8,24},{10,26},{12,28},{14,30},{16,0},... | collective-permute-start | bytes 245768 | tf_op jit(solution)/shard_map/ppermute | solution.py:50
  78.4 1.9 %collective-permute-done.12 = bf16[2,16,2560]{2,1,0:T(8,128)(2,1)S(1)} collective-permute-done((bf16[2,16,2560]{2,1,0:T(8,128)(2,1)S(1)}, bf16[2,16,2560]{2,1,0:T(8,128)(2,1)S(1)}, u32[]{:S(2)}, u32[]{:S(2)}) %collective-permute-start.12) | collective-permute-done | bytes 163872 | tf_op jit(solution)/shard_map/ppermute | solution.py:50
  80.3 2.6 %collective-permute-start.13 = (bf16[1,16,2560]{2,1,0:T(8,128)(2,1)S(1)}, bf16[1,16,2560]{2,1,0:T(8,128)(2,1)S(1)}, u32[]{:S(2)}, u32[]{:S(2)}) collective-permute-start(bf16[1,16,2560]{2,1,0:T(8,128)(2,1)S(1)} %dynamic-slice_convert_fusion.6), channel_id=1, source_target_pairs={{0,16},{2,18},{4,20},{6,22},{8,24},{10,26},{12,28},{14,30},{16,0},... | collective-permute-start | bytes 245768 | tf_op jit(solution)/shard_map/ppermute | solution.py:50
  83.0 2.9 %collective-permute-done.13 = bf16[1,16,2560]{2,1,0:T(8,128)(2,1)S(1)} collective-permute-done((bf16[1,16,2560]{2,1,0:T(8,128)(2,1)S(1)}, bf16[1,16,2560]{2,1,0:T(8,128)(2,1)S(1)}, u32[]{:S(2)}, u32[]{:S(2)}) %collective-permute-start.13) | collective-permute-done | bytes 81952 | tf_op jit(solution)/shard_map/ppermute | solution.py:50
  86.1 1.8 %collective-permute-start.21 = (bf16[2,16,2560]{2,1,0:T(8,128)(2,1)S(1)}, bf16[2,16,2560]{2,1,0:T(8,128)(2,1)S(1)}, u32[]{:S(2)}, u32[]{:S(2)}) collective-permute-start(bf16[2,16,2560]{2,1,0:T(8,128)(2,1)S(1)} %fusion.29), channel_id=1, source_target_pairs={{0,8},{2,10},{4,12},{6,14},{8,0},{10,2},{12,4},{14,6},{16,24},{18,... | collective-permute-start | bytes 491528 | tf_op jit(solution)/shard_map/ppermute | solution.py:50
  88.4 4.1 %collective-permute-done.21 = bf16[2,16,2560]{2,1,0:T(8,128)(2,1)S(1)} collective-permute-done((bf16[2,16,2560]{2,1,0:T(8,128)(2,1)S(1)}, bf16[2,16,2560]{2,1,0:T(8,128)(2,1)S(1)}, u32[]{:S(2)}, u32[]{:S(2)}) %collective-permute-start.21) | collective-permute-done | bytes 163872 | tf_op jit(solution)/shard_map/ppermute | solution.py:50
  92.6 3.4 %collective-permute-start.22 = (bf16[1,16,2560]{2,1,0:T(8,128)(2,1)S(1)}, bf16[1,16,2560]{2,1,0:T(8,128)(2,1)S(1)}, u32[]{:S(2)}, u32[]{:S(2)}) collective-permute-start(bf16[1,16,2560]{2,1,0:T(8,128)(2,1)S(1)} %dynamic-slice_convert_fusion.5), channel_id=1, source_target_pairs={{0,16},{2,18},{4,20},{6,22},{8,24},{10,26},{12,28},{14,30},{16,0},... | collective-permute-start | bytes 245768 | tf_op jit(solution)/shard_map/ppermute | solution.py:50
  96.0 1.7 %collective-permute-start.26 = (bf16[1,16,2560]{2,1,0:T(8,128)(2,1)S(1)}, bf16[1,16,2560]{2,1,0:T(8,128)(2,1)S(1)}, u32[]{:S(2)}, u32[]{:S(2)}) collective-permute-start(bf16[1,16,2560]{2,1,0:T(8,128)(2,1)S(1)} %dynamic-slice_convert_fusion.4), channel_id=1, source_target_pairs={{0,16},{2,18},{4,20},{6,22},{8,24},{10,26},{12,28},{14,30},{16,0},... | collective-permute-start | bytes 245768 | tf_op jit(solution)/shard_map/ppermute | solution.py:50
  97.7 0.7 collective-permute-done.22
  98.4 3.0 %collective-permute-done.26 = bf16[1,16,2560]{2,1,0:T(8,128)(2,1)S(1)} collective-permute-done((bf16[1,16,2560]{2,1,0:T(8,128)(2,1)S(1)}, bf16[1,16,2560]{2,1,0:T(8,128)(2,1)S(1)}, u32[]{:S(2)}, u32[]{:S(2)}) %collective-permute-start.26) | collective-permute-done | bytes 81952 | tf_op jit(solution)/shard_map/ppermute | solution.py:50
  101.5 0.8 copy-done.1
  (81 shorter events, 6.4 us)
Async XLA Ops:
  0.0 1.7 %copy-start = (bf16[1792,512]{1,0:T(8,128)(2,1)S(1)}, bf16[1792,512]{1,0:T(8,128)(2,1)}, u32[]{:S(2)}) copy-start(bf16[1792,512]{1,0:T(8,128)(2,1)} %param.6) | copy-start | bytes 5505028
  5.3 4.2 %copy-start.2 = (s32[512,1]{0,1:T(1,128)S(1)}, s32[512,1]{0,1:T(1,128)}, u32[]{:S(2)}) copy-start(s32[512,1]{0,1:T(1,128)} %param.8) | copy-start | bytes 6148
  7.2 40.7 %slice-start = ((s8[5242880]{0:T(1024)(128)(4,1)}), s8[1048576]{0:T(1024)(128)(4,1)S(1)}, s32[]{:S(2)}) async-start(s8[5242880]{0:T(1024)(128)(4,1)} %bitcast.146), calls=%async_computation | async-start | bytes 2097152
  9.9 4.9 %collective-permute-start.1 = (f32[17,256]{1,0:T(8,128)S(1)}, f32[17,256]{1,0:T(8,128)S(1)}, u32[]{:S(2)}, u32[]{:S(2)}) collective-permute-start(f32[17,256]{1,0:T(8,128)S(1)} %pad_maximum_fusion), channel_id=1, source_target_pairs={{0,1},{1,0},{2,3},{3,2},{4,5},{5,4},{6,7},{7,6},{8,9},{9,8},{10,11... | collective-permute-start | bytes 52232 | tf_op jit(solution)/shard_map/ppermute | solution.py:83
  16.2 1.2 %collective-permute-start.2 = (f32[16,384]{1,0:T(8,128)S(1)}, f32[16,384]{1,0:T(8,128)S(1)}, u32[]{:S(2)}, u32[]{:S(2)}) collective-permute-start(f32[16,384]{1,0:T(8,128)S(1)} %pad_maximum_fusion.1), channel_id=1, source_target_pairs={{0,2},{2,0},{4,6},{6,4},{8,10},{10,8},{12,14},{14,12},{16,18},{18,... | collective-permute-start | bytes 73736 | tf_op jit(solution)/shard_map/ppermute | solution.py:30
  17.4 3.8 %collective-permute-start.3 = (f32[16,384]{1,0:T(8,128)S(1)}, f32[16,384]{1,0:T(8,128)S(1)}, u32[]{:S(2)}, u32[]{:S(2)}) collective-permute-start(f32[16,384]{1,0:T(8,128)S(1)} %fusion.73), channel_id=1, source_target_pairs={{0,4},{2,6},{4,0},{6,2},{8,12},{10,14},{12,8},{14,10},{16,20},{18,... | collective-permute-start | bytes 73736 | tf_op jit(solution)/shard_map/ppermute | solution.py:30
  21.3 4.4 %collective-permute-start.4 = (f32[16,384]{1,0:T(8,128)S(1)}, f32[16,384]{1,0:T(8,128)S(1)}, u32[]{:S(2)}, u32[]{:S(2)}) collective-permute-start(f32[16,384]{1,0:T(8,128)S(1)} %add.203), channel_id=1, source_target_pairs={{0,8},{2,10},{4,12},{6,14},{8,0},{10,2},{12,4},{14,6},{16,24},{18,... | collective-permute-start | bytes 73736 | tf_op jit(solution)/shard_map/ppermute | solution.py:30
  24.1 7.6 %collective-permute-start = (bf16[16,16,512]{2,1,0:T(8,128)(2,1)}, bf16[16,16,512]{2,1,0:T(8,128)(2,1)S(1)}, u32[]{:S(2)}, u32[]{:S(2)}) collective-permute-start(bf16[16,16,512]{2,1,0:T(8,128)(2,1)} %fusion.18), channel_id=1, source_target_pairs={{0,1},{1,0},{2,3},{3,2},{4,5},{5,4},{6,7},{7,6},{8,9},{9,8},{10,11... | collective-permute-start | bytes 786440 | tf_op jit(solution)/shard_map/ppermute | solution.py:85
  25.6 4.8 %collective-permute-start.5 = (f32[16,384]{1,0:T(8,128)S(1)}, f32[16,384]{1,0:T(8,128)S(1)}, u32[]{:S(2)}, u32[]{:S(2)}) collective-permute-start(f32[16,384]{1,0:T(8,128)S(1)} %add.204), channel_id=1, source_target_pairs={{0,16},{2,18},{4,20},{6,22},{8,24},{10,26},{12,28},{14,30},{16,0},... | collective-permute-start | bytes 73736 | tf_op jit(solution)/shard_map/ppermute | solution.py:30
  33.0 6.4 %collective-permute-start.14 = (bf16[16,16,512]{2,1,0:T(8,128)(2,1)S(1)}, bf16[16,16,512]{2,1,0:T(8,128)(2,1)S(1)}, u32[]{:S(2)}, u32[]{:S(2)}) collective-permute-start(bf16[16,16,512]{2,1,0:T(8,128)(2,1)S(1)} %get-tuple-element.11), channel_id=1, source_target_pairs={{0,1},{1,0},{2,3},{3,2},{4,5},{5,4},{6,7},{7,6},{8,9},{9,8},{10,11... | collective-permute-start | bytes 786440 | tf_op jit(solution)/shard_map/ppermute | solution.py:101
  34.4 13.5 %slice-start.1 = ((s8[5242880]{0:T(1024)(128)(4,1)}), s8[4194304]{0:T(1024)(128)(4,1)S(1)}, s32[]{:S(2)}) async-start(s8[5242880]{0:T(1024)(128)(4,1)} %bitcast.146), calls=%async_computation.1 | async-start | bytes 8388608
  39.6 2.4 %collective-permute-start.15 = (f32[2,16,16]{2,1,0:T(8,128)S(1)}, f32[2,16,16]{2,1,0:T(8,128)S(1)}, u32[]{:S(2)}, u32[]{:S(2)}) collective-permute-start(f32[2,16,16]{2,1,0:T(8,128)S(1)} %pad_maximum_fusion.2), channel_id=1, source_target_pairs={{0,2},{2,0},{4,6},{6,4},{8,10},{10,8},{12,14},{14,12},{16,18},{18,... | collective-permute-start | bytes 6152 | tf_op jit(solution)/shard_map/ppermute | solution.py:30
  41.9 4.4 %collective-permute-start.16 = (f32[2,16,16]{2,1,0:T(8,128)S(1)}, f32[2,16,16]{2,1,0:T(8,128)S(1)}, u32[]{:S(2)}, u32[]{:S(2)}) collective-permute-start(f32[2,16,16]{2,1,0:T(8,128)S(1)} %fusion.74), channel_id=1, source_target_pairs={{0,4},{2,6},{4,0},{6,2},{8,12},{10,14},{12,8},{14,10},{16,20},{18,... | collective-permute-start | bytes 6152 | tf_op jit(solution)/shard_map/ppermute | solution.py:30
  45.8 9.7 %collective-permute-start.6 = (bf16[8,16,2560]{2,1,0:T(8,128)(2,1)S(1)}, bf16[8,16,2560]{2,1,0:T(8,128)(2,1)S(1)}, u32[]{:S(2)}, u32[]{:S(2)}) collective-permute-start(bf16[8,16,2560]{2,1,0:T(8,128)(2,1)S(1)} %convolution_convert_fusion.3), channel_id=1, source_target_pairs={{0,2},{2,0},{4,6},{6,4},{8,10},{10,8},{12,14},{14,12},{16,18},{18,... | collective-permute-start | bytes 1966088 | tf_op jit(solution)/shard_map/ppermute | solution.py:45
  46.1 10.9 %collective-permute-start.10 = (bf16[8,16,2560]{2,1,0:T(8,128)(2,1)S(1)}, bf16[8,16,2560]{2,1,0:T(8,128)(2,1)S(1)}, u32[]{:S(2)}, u32[]{:S(2)}) collective-permute-start(bf16[8,16,2560]{2,1,0:T(8,128)(2,1)S(1)} %convolution_convert_fusion.2), channel_id=1, source_target_pairs={{0,2},{2,0},{4,6},{6,4},{8,10},{10,8},{12,14},{14,12},{16,18},{18,... | collective-permute-start | bytes 1966088 | tf_op jit(solution)/shard_map/ppermute | solution.py:45
  46.4 3.8 %collective-permute-start.17 = (f32[2,16,16]{2,1,0:T(8,128)S(1)}, f32[2,16,16]{2,1,0:T(8,128)S(1)}, u32[]{:S(2)}, u32[]{:S(2)}) collective-permute-start(f32[2,16,16]{2,1,0:T(8,128)S(1)} %fusion.81), channel_id=1, source_target_pairs={{0,8},{2,10},{4,12},{6,14},{8,0},{10,2},{12,4},{14,6},{16,24},{18,... | collective-permute-start | bytes 6152 | tf_op jit(solution)/shard_map/ppermute | solution.py:30
  50.2 4.6 %collective-permute-start.18 = (f32[2,16,16]{2,1,0:T(8,128)S(1)}, f32[2,16,16]{2,1,0:T(8,128)S(1)}, u32[]{:S(2)}, u32[]{:S(2)}) collective-permute-start(f32[2,16,16]{2,1,0:T(8,128)S(1)} %add.224), channel_id=1, source_target_pairs={{0,16},{2,18},{4,20},{6,22},{8,24},{10,26},{12,28},{14,30},{16,0},... | collective-permute-start | bytes 6152 | tf_op jit(solution)/shard_map/ppermute | solution.py:30
  53.4 5.5 %collective-permute-start.19 = (bf16[8,16,2560]{2,1,0:T(8,128)(2,1)S(1)}, bf16[8,16,2560]{2,1,0:T(8,128)(2,1)S(1)}, u32[]{:S(2)}, u32[]{:S(2)}) collective-permute-start(bf16[8,16,2560]{2,1,0:T(8,128)(2,1)S(1)} %convolution_convert_fusion.1), channel_id=1, source_target_pairs={{0,2},{2,0},{4,6},{6,4},{8,10},{10,8},{12,14},{14,12},{16,18},{18,... | collective-permute-start | bytes 1966088 | tf_op jit(solution)/shard_map/ppermute | solution.py:45
  53.5 6.9 %collective-permute-start.23 = (bf16[8,16,2560]{2,1,0:T(8,128)(2,1)S(1)}, bf16[8,16,2560]{2,1,0:T(8,128)(2,1)S(1)}, u32[]{:S(2)}, u32[]{:S(2)}) collective-permute-start(bf16[8,16,2560]{2,1,0:T(8,128)(2,1)S(1)} %convolution_convert_fusion), channel_id=1, source_target_pairs={{0,2},{2,0},{4,6},{6,4},{8,10},{10,8},{12,14},{14,12},{16,18},{18,... | collective-permute-start | bytes 1966088 | tf_op jit(solution)/shard_map/ppermute | solution.py:45
  56.1 10.7 %collective-permute-start.7 = (bf16[4,16,2560]{2,1,0:T(8,128)(2,1)S(1)}, bf16[4,16,2560]{2,1,0:T(8,128)(2,1)S(1)}, u32[]{:S(2)}, u32[]{:S(2)}) collective-permute-start(bf16[4,16,2560]{2,1,0:T(8,128)(2,1)S(1)} %fusion.21), channel_id=1, source_target_pairs={{0,4},{2,6},{4,0},{6,2},{8,12},{10,14},{12,8},{14,10},{16,20},{18,... | collective-permute-start | bytes 983048 | tf_op jit(solution)/shard_map/ppermute | solution.py:50
  57.6 16.2 %collective-permute-start.11 = (bf16[4,16,2560]{2,1,0:T(8,128)(2,1)S(1)}, bf16[4,16,2560]{2,1,0:T(8,128)(2,1)S(1)}, u32[]{:S(2)}, u32[]{:S(2)}) collective-permute-start(bf16[4,16,2560]{2,1,0:T(8,128)(2,1)S(1)} %fusion.22), channel_id=1, source_target_pairs={{0,4},{2,6},{4,0},{6,2},{8,12},{10,14},{12,8},{14,10},{16,20},{18,... | collective-permute-start | bytes 983048 | tf_op jit(solution)/shard_map/ppermute | solution.py:50
  59.4 26.6 %collective-permute-start.20 = (bf16[4,16,2560]{2,1,0:T(8,128)(2,1)S(1)}, bf16[4,16,2560]{2,1,0:T(8,128)(2,1)S(1)}, u32[]{:S(2)}, u32[]{:S(2)}) collective-permute-start(bf16[4,16,2560]{2,1,0:T(8,128)(2,1)S(1)} %fusion.23), channel_id=1, source_target_pairs={{0,4},{2,6},{4,0},{6,2},{8,12},{10,14},{12,8},{14,10},{16,20},{18,... | collective-permute-start | bytes 983048 | tf_op jit(solution)/shard_map/ppermute | solution.py:50
  60.9 27.0 %collective-permute-start.24 = (bf16[4,16,2560]{2,1,0:T(8,128)(2,1)S(1)}, bf16[4,16,2560]{2,1,0:T(8,128)(2,1)S(1)}, u32[]{:S(2)}, u32[]{:S(2)}) collective-permute-start(bf16[4,16,2560]{2,1,0:T(8,128)(2,1)S(1)} %fusion.24), channel_id=1, source_target_pairs={{0,4},{2,6},{4,0},{6,2},{8,12},{10,14},{12,8},{14,10},{16,20},{18,... | collective-permute-start | bytes 983048 | tf_op jit(solution)/shard_map/ppermute | solution.py:50
  66.8 8.5 %collective-permute-start.8 = (bf16[2,16,2560]{2,1,0:T(8,128)(2,1)S(1)}, bf16[2,16,2560]{2,1,0:T(8,128)(2,1)S(1)}, u32[]{:S(2)}, u32[]{:S(2)}) collective-permute-start(bf16[2,16,2560]{2,1,0:T(8,128)(2,1)S(1)} %fusion.27), channel_id=1, source_target_pairs={{0,8},{2,10},{4,12},{6,14},{8,0},{10,2},{12,4},{14,6},{16,24},{18,... | collective-permute-start | bytes 491528 | tf_op jit(solution)/shard_map/ppermute | solution.py:50
  73.9 6.4 %collective-permute-start.12 = (bf16[2,16,2560]{2,1,0:T(8,128)(2,1)S(1)}, bf16[2,16,2560]{2,1,0:T(8,128)(2,1)S(1)}, u32[]{:S(2)}, u32[]{:S(2)}) collective-permute-start(bf16[2,16,2560]{2,1,0:T(8,128)(2,1)S(1)} %fusion.28), channel_id=1, source_target_pairs={{0,8},{2,10},{4,12},{6,14},{8,0},{10,2},{12,4},{14,6},{16,24},{18,... | collective-permute-start | bytes 491528 | tf_op jit(solution)/shard_map/ppermute | solution.py:50
  75.5 7.5 %collective-permute-start.9 = (bf16[1,16,2560]{2,1,0:T(8,128)(2,1)S(1)}, bf16[1,16,2560]{2,1,0:T(8,128)(2,1)S(1)}, u32[]{:S(2)}, u32[]{:S(2)}) collective-permute-start(bf16[1,16,2560]{2,1,0:T(8,128)(2,1)S(1)} %dynamic-slice_convert_fusion.7), channel_id=1, source_target_pairs={{0,16},{2,18},{4,20},{6,22},{8,24},{10,26},{12,28},{14,30},{16,0},... | collective-permute-start | bytes 245768 | tf_op jit(solution)/shard_map/ppermute | solution.py:50
  80.3 5.5 %collective-permute-start.13 = (bf16[1,16,2560]{2,1,0:T(8,128)(2,1)S(1)}, bf16[1,16,2560]{2,1,0:T(8,128)(2,1)S(1)}, u32[]{:S(2)}, u32[]{:S(2)}) collective-permute-start(bf16[1,16,2560]{2,1,0:T(8,128)(2,1)S(1)} %dynamic-slice_convert_fusion.6), channel_id=1, source_target_pairs={{0,16},{2,18},{4,20},{6,22},{8,24},{10,26},{12,28},{14,30},{16,0},... | collective-permute-start | bytes 245768 | tf_op jit(solution)/shard_map/ppermute | solution.py:50
  86.1 6.4 %collective-permute-start.21 = (bf16[2,16,2560]{2,1,0:T(8,128)(2,1)S(1)}, bf16[2,16,2560]{2,1,0:T(8,128)(2,1)S(1)}, u32[]{:S(2)}, u32[]{:S(2)}) collective-permute-start(bf16[2,16,2560]{2,1,0:T(8,128)(2,1)S(1)} %fusion.29), channel_id=1, source_target_pairs={{0,8},{2,10},{4,12},{6,14},{8,0},{10,2},{12,4},{14,6},{16,24},{18,... | collective-permute-start | bytes 491528 | tf_op jit(solution)/shard_map/ppermute | solution.py:50
  88.1 7.9 %collective-permute-start.25 = (bf16[2,16,2560]{2,1,0:T(8,128)(2,1)S(1)}, bf16[2,16,2560]{2,1,0:T(8,128)(2,1)S(1)}, u32[]{:S(2)}, u32[]{:S(2)}) collective-permute-start(bf16[2,16,2560]{2,1,0:T(8,128)(2,1)S(1)} %fusion.30), channel_id=1, source_target_pairs={{0,8},{2,10},{4,12},{6,14},{8,0},{10,2},{12,4},{14,6},{16,24},{18,... | collective-permute-start | bytes 491528 | tf_op jit(solution)/shard_map/ppermute | solution.py:50
  92.6 5.8 %collective-permute-start.22 = (bf16[1,16,2560]{2,1,0:T(8,128)(2,1)S(1)}, bf16[1,16,2560]{2,1,0:T(8,128)(2,1)S(1)}, u32[]{:S(2)}, u32[]{:S(2)}) collective-permute-start(bf16[1,16,2560]{2,1,0:T(8,128)(2,1)S(1)} %dynamic-slice_convert_fusion.5), channel_id=1, source_target_pairs={{0,16},{2,18},{4,20},{6,22},{8,24},{10,26},{12,28},{14,30},{16,0},... | collective-permute-start | bytes 245768 | tf_op jit(solution)/shard_map/ppermute | solution.py:50
  96.0 5.4 %collective-permute-start.26 = (bf16[1,16,2560]{2,1,0:T(8,128)(2,1)S(1)}, bf16[1,16,2560]{2,1,0:T(8,128)(2,1)S(1)}, u32[]{:S(2)}, u32[]{:S(2)}) collective-permute-start(bf16[1,16,2560]{2,1,0:T(8,128)(2,1)S(1)} %dynamic-slice_convert_fusion.4), channel_id=1, source_target_pairs={{0,16},{2,18},{4,20},{6,22},{8,24},{10,26},{12,28},{14,30},{16,0},... | collective-permute-start | bytes 245768 | tf_op jit(solution)/shard_map/ppermute | solution.py:50
  101.5 0.8 copy-start.1

commit v2 on v0

v2 whole, which is shorter than its diff:
```python
import functools

import jax
import jax.numpy as jnp
from jax import lax
from jax.experimental import pallas as pl
from jax.experimental.pallas import tpu as pltpu
from jax.sharding import PartitionSpec as P


COHORTS = 16
LANES = 128
BF16, F32 = jnp.bfloat16, jnp.float32
EXACT = lax.Precision.HIGHEST


def flip(size, stride):
    return [(i, i ^ stride) for i in range(size)]


def shift(size, step):
    return [(i, (i + step) % size) for i in range(size)]


def strides(size):
    return [1 << bit for bit in range(size.bit_length() - 1)]


def pick(array, index, axis):
    return lax.dynamic_index_in_dim(array, index, axis, keepdims=False)


def in_hbm(array):
    return pltpu.with_memory_space_constraint(array, pltpu.HBM)


def all_sum(value, size):
    for stride in strides(size):
        value = value + lax.ppermute(value, "samp", flip(size, stride))
    return value


def member_of(cohort, kind=F32):
    shape = (COHORTS, cohort.shape[-1])
    return (cohort == lax.broadcasted_iota(jnp.int32, shape, 0)).astype(kind)


def cohort_sums(member, values):
    values = values.reshape(-1, values.shape[-1])
    return lax.dot_general(
        member, values, (((1,), (1,)), ((), ())), precision=EXACT, preferred_element_type=F32
    )


def of_members(table, member):
    return lax.dot_general(
        table, member, (((0,), (0,)), ((), ())), precision=EXACT, preferred_element_type=F32
    )


def thirds(values):
    high = values.astype(BF16)
    values = values - high.astype(F32)
    mid = values.astype(BF16)
    return high, mid, (values - mid.astype(F32)).astype(BF16)


def score_kernel(cuts, where_ref, weights_ref, dosages_ref, prior_ref, cohort_ref, *refs):
    *refs, weights, dosages, prior, cohort, acc, sems = refs
    part = where_ref[1]
    size, parts, rows, samples = acc.shape
    share = size // parts
    (own_ref, *sent_refs), sums_refs = refs[:parts], refs[parts:]
    width = size * rows
    copies = []
    for k, (at, count) in enumerate(cuts):
        copies.append(
            (
                pltpu.make_async_copy(
                    weights_ref.at[pl.ds(at, count)], weights.at[pl.ds(at, count)], sems.at[0, k]
                ),
                pltpu.make_async_copy(
                    dosages_ref.at[:, pl.ds(at, count)],
                    dosages.at[:, pl.ds(at, count)],
                    sems.at[1, k],
                ),
            )
        )
        copies[k][0].start()
        copies[k][1].start()
    extra = pltpu.make_async_copy(prior_ref, prior, sems.at[2, 0])
    extra.start()
    known = pltpu.make_async_copy(cohort_ref, cohort, sems.at[2, 1])
    known.start()
    for k, (at, count) in enumerate(cuts):
        copies[k][0].wait()
        copies[k][1].wait()
        product = lax.dot_general(
            weights[pl.ds(at, count)],
            dosages[:, pl.ds(at, count)],
            (((0,), (1,)), ((), ())),
            preferred_element_type=F32,
        ).reshape(acc.shape)
        if k == 0:
            acc[...] = product
        else:
            acc[...] += product
    known.wait()
    member = member_of(cohort[...], BF16)
    extra.wait()
    acc[pl.ds(part * share, share)] += prior[...].T.reshape(share, parts, rows, samples)

    def sums_of(values):
        pieces = thirds(values.reshape(size * rows, samples))
        return sum(
            lax.dot_general(member, x, (((1,), (1,)), ((), ())), preferred_element_type=F32)
            for x in pieces
        )

    values = acc[:, part]
    own_ref[...] = values
    sums_refs[0][:, :width] = sums_of(values)
    counts = jnp.sum(member.astype(F32), axis=1, keepdims=True)
    sums_refs[0][:, width:] = jnp.broadcast_to(counts, (COHORTS, LANES))
    for other in range(1, parts):
        values = acc[:, lax.rem(part + other, parts)]
        sums_refs[other][:, :width] = sums_of(values)
        sums_refs[other][:, width:] = jnp.zeros((COHORTS, LANES), F32)
        mean = jnp.mean(values, axis=2, keepdims=True)
        sent_refs[other - 1][...] = (values - mean).astype(BF16)


def center_kernel(own_ref, total_ref, cohort_ref, *refs):
    *others, out_ref = refs
    size, rows, samples = own_ref.shape
    width = size * rows
    table = -total_ref[:, :width] / total_ref[:, width : width + 1]
    scores = own_ref[...]
    for got_ref, theirs_ref in zip(others[::2], others[1::2]):
        scores += got_ref[...].astype(F32)
        table += jnp.sum(theirs_ref[:, :width], axis=0, keepdims=True) / samples
    member = member_of(cohort_ref[...], BF16)
    scores += lax.dot_general(
        jnp.concatenate(thirds(table), axis=0),
        jnp.concatenate([member] * 3, axis=0),
        (((0,), (0,)), ((), ())),
        preferred_element_type=F32,
    ).reshape(scores.shape)
    out_ref[...] = scores.astype(BF16)


def local_scores(dosages, weights, prior, cohort, where, size, parts):
    samples, variants = dosages.shape
    width = prior.shape[1]
    rows = width // size
    if rows % 16 == 0 and samples % LANES == 0 and variants % 256 == 0:
        step = min(512, variants)
        cuts = [(at, min(step, variants - at)) for at in range(0, variants, step)]
        vmem = pl.BlockSpec(memory_space=pltpu.VMEM)
        hbm = pl.BlockSpec(memory_space=pltpu.HBM)
        part_shape = (size, rows, samples)
        out = pl.pallas_call(
            functools.partial(score_kernel, cuts),
            out_shape=[
                pltpu.VMEM(part_shape, F32),
                *[pltpu.VMEM(part_shape, BF16)] * (parts - 1),
                *[pltpu.VMEM((COHORTS, width + LANES), F32)] * parts,
            ],
            in_specs=[pl.BlockSpec(memory_space=pltpu.SMEM), hbm, hbm, hbm, hbm],
            out_specs=[vmem] * (2 * parts),
            scratch_shapes=[
                pltpu.VMEM((variants, width * parts), BF16),
                pltpu.VMEM((samples, variants), BF16),
                pltpu.VMEM((samples, width), F32),
                pltpu.VMEM((1, samples), jnp.int32),
                pltpu.VMEM((size, parts, rows, samples), F32),
                pltpu.SemaphoreType.DMA((3, len(cuts))),
            ],
            compiler_params=pltpu.CompilerParams(vmem_limit_bytes=16 << 20),
            name="scores",
        )(where, *map(in_hbm, (weights, dosages, prior, cohort)))
        return out[0], out[1:parts], out[parts:]
    part = where[1]
    scores = lax.dot_general(
        weights, dosages, (((0,), (1,)), ((), ())), preferred_element_type=F32
    ).reshape(size, parts, rows, samples)
    at = part * (size // parts)
    own = lax.dynamic_slice_in_dim(scores, at, size // parts, 0)
    own = own + prior.T.reshape(size // parts, parts, rows, samples)
    scores = lax.dynamic_update_slice_in_dim(scores, own, at, 0)
    by_part = [pick(scores, (part + other) % parts, 1) for other in range(parts)]
    member = member_of(cohort)
    counts = jnp.broadcast_to(jnp.sum(member, axis=1, keepdims=True), (COHORTS, LANES))
    sums = [
        jnp.concatenate([cohort_sums(member, x), counts * (k == 0)], axis=1)
        for k, x in enumerate(by_part)
    ]
    sent = [(x - jnp.mean(x, axis=2, keepdims=True)).astype(BF16) for x in by_part[1:]]
    return by_part[0], sent, sums


def center(own, got, theirs, total, cohort):
    size, rows, samples = own.shape
    if rows % 16 == 0 and samples % LANES == 0:
        others = [x for pair in zip(got, theirs) for x in pair]
        return pl.pallas_call(
            center_kernel,
            out_shape=pltpu.VMEM(own.shape, BF16),
            compiler_params=pltpu.CompilerParams(vmem_limit_bytes=8 << 20),
            name="center",
        )(own, total, cohort, *others)
    width = size * rows
    table = -total[:, :width] / total[:, width : width + 1]
    table = table + jnp.sum(sum(theirs)[:, :width], axis=0)[None, :] / samples
    table = of_members(table, member_of(cohort)).reshape(own.shape)
    return (own + sum(x.astype(F32) for x in got) + table).astype(BF16)


def stage_kernel(source_ref, out_ref, sem):
    copy = pltpu.make_async_copy(source_ref, out_ref, sem)
    copy.start()
    copy.wait()


def stage(array):
    if array.size * array.dtype.itemsize > 6 << 20:
        return array
    return pl.pallas_call(
        stage_kernel,
        out_shape=pltpu.VMEM(array.shape, array.dtype),
        in_specs=[pl.BlockSpec(memory_space=pltpu.HBM)],
        out_specs=pl.BlockSpec(memory_space=pltpu.VMEM),
        scratch_shapes=[pltpu.SemaphoreType.DMA],
        compiler_params=pltpu.CompilerParams(vmem_limit_bytes=1 << 20),
        name="stage",
    )(in_hbm(array))


def product_kernel(cuts, squares, where_ref, standard_ref, expression_ref, sent_ref, mine_ref):
    bit = where_ref[0] & 1
    half, _, rows, samples = standard_ref.shape
    sent = standard_ref[:, 1 - bit].reshape(half * rows, samples)
    mine = standard_ref[:, bit].reshape(half * rows, samples)
    if squares:
        end = sum(cuts[-1][::2])
        first = lax.broadcasted_iota(jnp.int32, (half * rows, LANES), 1) < LANES // 2
        total = jnp.sum(sent.astype(F32) ** 2, axis=1, keepdims=True)
        high = total.astype(BF16).astype(F32)
        sent_ref[:, end:] = jnp.where(first, high, total - high).astype(BF16)
        total = jnp.sum(mine.astype(F32) ** 2, axis=1, keepdims=True)
        mine_ref[:, end:] = jnp.where(first, total, 0.0)
    both = jnp.concatenate([sent, mine], axis=0)
    for at, start, count in cuts:
        block = expression_ref[:, start : start + count]
        total = jnp.dot(both, block, preferred_element_type=F32)
        sent_ref[:, at : at + count] = total[: half * rows].astype(BF16)
        mine_ref[:, at : at + count] = total[half * rows :]


def products(standard, expression, where, at, count, squares):
    size, rows, samples = standard.shape
    halves = standard.reshape(size // 2, 2, rows, samples)
    if rows % 16 == 0 and samples % LANES == 0 and count % LANES == 0:
        step = 512
        cuts = [(k, at + k, min(step, count - k)) for k in range(0, count, step)]
        shape = (size // 2 * rows, count + LANES * squares)
        vmem = pl.BlockSpec(memory_space=pltpu.VMEM)
        return pl.pallas_call(
            functools.partial(product_kernel, cuts, squares),
            out_shape=[pltpu.VMEM(shape, BF16), pltpu.VMEM(shape, F32)],
            in_specs=[pl.BlockSpec(memory_space=pltpu.SMEM), vmem, vmem],
            out_specs=[vmem, vmem],
            compiler_params=pltpu.CompilerParams(vmem_limit_bytes=12 << 20),
        )(where, halves, expression)
    expression = expression[:, at : at + count]
    results = []
    place = where[0]
    for k in (1 - place & 1, place & 1):
        lhs = pick(halves, k, 1).reshape(-1, samples)
        result = jnp.dot(lhs, expression, preferred_element_type=F32)
        if squares:
            total = jnp.sum(lhs.astype(F32) ** 2, axis=1, keepdims=True)
            total = jnp.broadcast_to(total, (total.shape[0], LANES))
            first = jnp.arange(LANES) < LANES // 2
            if not results:
                high = lax.reduce_precision(total, 8, 7)
                total = jnp.where(first, high, total - high)
            else:
                total = jnp.where(first, total, 0.0)
            result = jnp.concatenate([result, total], axis=1)
        results.append(result)
    return results[0].astype(BF16), results[1]


def fold_kernel(shift, where_ref, mine_ref, got_ref, sent_ref, kept_ref):
    bit = (where_ref[0] >> shift) & 1
    sent_ref[...] = (mine_ref[:, 1 - bit] + got_ref[:, 1 - bit].astype(F32)).astype(BF16)
    kept_ref[...] = mine_ref[:, bit] + got_ref[:, bit].astype(F32)


def fold(mine, got, where, stride):
    before, _, rows, width = mine.shape
    if rows % 16 == 0 and width % LANES == 0:
        vmem = pl.BlockSpec(memory_space=pltpu.VMEM)
        return pl.pallas_call(
            functools.partial(fold_kernel, stride.bit_length() - 1),
            out_shape=[pltpu.VMEM((before, rows, width), kind) for kind in (BF16, F32)],
            in_specs=[pl.BlockSpec(memory_space=pltpu.SMEM), vmem, vmem],
            out_specs=[vmem, vmem],
            compiler_params=pltpu.CompilerParams(vmem_limit_bytes=4 << 20),
        )(where, mine, got)
    total = mine + got.astype(F32)
    bit = (where[0] // stride) & 1
    return pick(total, 1 - bit, 1).astype(BF16), pick(total, bit, 1)


def scatter_sum(standard, expression, where, size, chunk):
    at, count, order = chunk
    rows = standard.shape[1]
    sent, mine = products(standard, expression, where, at, count, at == 0)
    width = sent.shape[1]
    left = strides(size)[::-1]
    for stride, coming in zip(order, [*order[1:], None]):
        left.remove(stride)
        got = lax.ppermute(sent, "samp", flip(size, stride))
        if coming is None:
            return mine.reshape(rows, width), got.reshape(rows, width)
        axis = left.index(coming)
        shape = (2**axis, 2, 2 ** (len(left) - axis - 1) * rows, width)
        sent, mine = fold(mine.reshape(shape), got.reshape(shape), where, coming)


def finish_kernel(plan, everyone, where_ref, *refs):
    *refs, out_ref = refs
    parts = len(plan)
    terms = iter(zip(refs[::2], refs[1::2]))
    for k, chunks in enumerate(plan):
        part = lax.rem(where_ref[1] + parts - k, parts)
        for at, count, _ in chunks:
            mine, got = next(terms)
            total = mine[...] + got[...].astype(F32)
            if at == 0:
                middle = count + LANES // 2
                squares = total[:, count : count + 1] + total[:, middle : middle + 1]
                spread = lax.rsqrt(squares / everyone + 1e-06) / everyone
            out_ref[part, :, at : at + count] = total[:, :count] * spread


def finish(cross, plan, where, everyone):
    rows = cross[0][0].shape[0]
    genes = sum(chunk[1] for chunk in plan[0])
    parts = len(plan)
    if rows % 16 == 0:
        vmem = pl.BlockSpec(memory_space=pltpu.VMEM)
        return pl.pallas_call(
            functools.partial(finish_kernel, plan, everyone),
            out_shape=jax.ShapeDtypeStruct((parts, rows, genes), F32),
            in_specs=[pl.BlockSpec(memory_space=pltpu.SMEM), *[vmem] * (2 * len(cross))],
            out_specs=vmem,
            compiler_params=pltpu.CompilerParams(vmem_limit_bytes=12 << 20),
            name="finish",
        )(where, *[x for pair in cross for x in pair])
    result = jnp.zeros((parts, rows, genes), F32)
    cross = iter([mine + got.astype(F32) for mine, got in cross])
    for k, chunks in enumerate(plan):
        totals = [next(cross) for _ in chunks]
        count = chunks[0][1]
        squares = totals[0][:, count] + totals[0][:, count + LANES // 2]
        spread = lax.rsqrt(squares / everyone + 1e-06) / everyone
        values = jnp.concatenate([totals[0][:, :count], *totals[1:]], axis=1) * spread[:, None]
        result = lax.dynamic_update_slice_in_dim(result, values[None], (where[1] - k) % parts, 0)
    return result


def chunk_plan(size, parts, genes):
    near = strides(size)
    late = [near[0], near[2], near[1], *near[3:]] if size >= 8 else near
    tiles = genes // LANES
    cut = tiles * 11 // 20 * LANES
    plan = [[(0, cut, near), (cut, genes - cut, near)]]
    for _ in range(1, parts):
        cut = tiles * 2 // 5 * LANES
        plan.append([(0, cut, near), (cut, genes - cut, late)])
    return plan


def shards(dosages, weights, prior, cohort, expression, *, size, parts):
    where = jnp.stack([lax.axis_index("samp"), lax.axis_index("var")]).astype(jnp.int32)
    samples, width = prior.shape
    rows = width // size
    genes = expression.shape[1]
    cohort = cohort.reshape(1, samples)

    own, sent, sums = local_scores(dosages, weights, prior, cohort, where, size, parts)
    theirs = [lax.ppermute(sums[k], "var", shift(parts, k)) for k in range(1, parts)]
    got = [lax.ppermute(sent[k - 1], "var", shift(parts, k)) for k in range(1, parts)]
    total = all_sum(sum(theirs, sums[0]), size)
    if rows % 16 == 0:
        expression = stage(expression)

    standard = [center(own, got, theirs, total, cohort)]
    for k in range(1, parts):
        standard.append(lax.ppermute(standard[0], "var", shift(parts, k)))

    plan = chunk_plan(size, parts, genes)
    cross = [
        scatter_sum(standard[k], expression, where, size, chunk)
        for k, chunks in enumerate(plan)
        for chunk in chunks
    ]
    return finish(cross, plan, where, samples * size).reshape(parts * rows, genes)


def solution(mesh):
    size, parts = mesh.shape["samp"], mesh.shape["var"]
    placed = (P("samp", "var"), P("var", None), P("samp", "var"), P("samp", None), P("samp", "var"))
    return jax.shard_map(
        functools.partial(shards, size=size, parts=parts),
        mesh=mesh,
        in_specs=placed,
        out_specs=P("samp", "var"),
        check_vma=False,
    )
```

time: 255 us -> 90.7 us (0.36)
  waiting for transfers between devices: 159 us -> 41.2 us
  blocking collectives: 61 us -> 0 us
  starting transfers between devices: 0.04 us -> 27.5 us
  Pallas kernels: 0 us -> 21.5 us
  between operations: 13.5 us -> 0.15 us
  matrix products: 13.1 us -> 0 us
  other arithmetic: 5.58 us -> 0.1 us
    reduce_scatter x1 -> x0, waiting for transfers between devices: 116 us -> none  [shards(): lax.psum_scatter(lax.dot_general(standard, expression, (((0,), (0,)), (()...]
    psum x1 -> x0, blocking collectives: 61 us -> none  [standardize(): sums, counts, raw_squares = lax.psum((sums, counts, raw_squares), 'samp')]
    psum x1 -> x0, waiting for transfers between devices: 42.8 us -> none  [shards(): scores = lax.psum(partial_value, 'var')]
    ppermute x0 -> x23, waiting for transfers between devices: none -> 41.2 us  [the longest x16 25.2 us: scatter_sum(): got = lax.ppermute(sent, 'samp', flip(size, stride))]
    ppermute x0 -> x23, starting transfers between devices: none -> 27.5 us  [the longest x16 16.2 us: scatter_sum(): got = lax.ppermute(sent, 'samp', flip(size, stride))]
    pallas_call x0 -> x20, Pallas kernels: none -> 21.5 us  [the longest x12 7.42 us: fold(): pl.pallas_call(functools.partial(fold_kernel, stride.bit_length() - 1), o...]
    dot_general x4 -> x0, matrix products: 13.1 us -> none  [the longest x1 8.05 us: shards(): lax.dot_general(standard, expression, (((0,), (0,)), ((), ())), preferred...]
    div x1 -> x0, other arithmetic: 2.58 us -> none  [shards(): return cross / total]
  transfers between devices with their start and end apart: 2 -> 23, of which waited for: 2 -> 13; matrix products, arithmetic and copies ran while one was open for 0% -> 0% of each run, Pallas kernels for 0% -> 15%
where the time goes in v2:
time: 90.7 us; the launch traced here: 90.5 us
  waiting for transfers between devices  41.2 us (45%)
  starting transfers between devices  27.5 us (30%)
  Pallas kernels  21.5 us (24%)
    ppermute x16, waiting for transfers between devices, scatter_sum(): got = lax.ppermute(sent, 'samp', flip(size, stride))  25.2 us
    ppermute x16, starting transfers between devices, scatter_sum(): got = lax.ppermute(sent, 'samp', flip(size, stride))  16.2 us
    pallas_call x12, Pallas kernels, fold(): pl.pallas_call(functools.partial(fold_kernel, stride.bit_length() - 1), o...  7.42 us
    ppermute x4, waiting for transfers between devices, all_sum(): value = value + lax.ppermute(value, 'samp', flip(size, stride))  7.12 us
    ppermute x1, waiting for transfers between devices, shards(): lax.ppermute(sums[k], 'var', shift(parts, k))  6.75 us
    ppermute x4, starting transfers between devices, all_sum(): value = value + lax.ppermute(value, 'samp', flip(size, stride))  6.45 us
    pallas_call x4, Pallas kernels, products(): pl.pallas_call(functools.partial(product_kernel, cuts, squares), out_shap...  5.55 us
    pallas_call x1, Pallas kernels, local_scores(): pl.pallas_call(functools.partial(score_kernel, cuts), out_shape=[pltpu.VM...  4.1 us
  transfers between devices with their start and end apart: 23, of which 13 were waited for; matrix products, arithmetic and copies ran while one was open for 0% of the time, Pallas kernels for 15%

profile of v2, /device:TPU:0, one launch (start us, length us, event | category | flops | bytes accessed | tf_op | source)
XLA Modules:
  0.0 90.5 jit_solution(4862898026068649248)
XLA Ops:
  0.1 4.1 %scores.1 = (f32[16,16,512]{2,1,0:T(8,128)S(1)}, bf16[16,16,512]{2,1,0:T(8,128)(2,1)S(1)}, f32[16,384]{1,0:T(8,128)S(1)}, f32[16,384]{1,0:T(8,128)S(1)}) custom-call(s32[2]{0:T(128)S(1)} %pad_add_fusion.where_ref, bf16[1792,512]{1,0:T(8,128)(2,1)} %weights_ref.1, bf16[512,1792]{1,0:T(8,128)(2,1)} %dosages_ref.1, f32[512,256]{1,0:T(8,128)} %prior_ref.1, ...), custom_call_target="tpu_custom_call" | custom-call | tf_op jit(solution)/shard_map/scores/pallas_call | solution.py:162
  4.2 3.0 %collective-permute-start.5 = (bf16[16,16,512]{2,1,0:T(8,128)(2,1)S(1)}, bf16[16,16,512]{2,1,0:T(8,128)(2,1)S(1)}, u32[]{:S(2)}, u32[]{:S(2)}) collective-permute-start(bf16[16,16,512]{2,1,0:T(8,128)(2,1)S(1)} %get-tuple-element.44), channel_id=1, source_target_pairs={{0,1},{1,0},{2,3},{3,2},{4,5},{5,4},{6,7},{7,6},{8,9},{9,8},{10,11... | collective-permute-start | bytes 786440 | tf_op jit(solution)/shard_map/ppermute | solution.py:396
  7.3 6.8 %collective-permute-done.refs_1_ = f32[16,384]{1,0:T(8,128)S(1)} collective-permute-done((f32[16,384]{1,0:T(8,128)S(1)}, f32[16,384]{1,0:T(8,128)S(1)}, u32[]{:S(2)}, u32[]{:S(2)}) %collective-permute-start) | collective-permute-done | bytes 24608 | tf_op jit(solution)/shard_map/ppermute | solution.py:395
  14.0 1.2 %collective-permute-done.1 = f32[16,384]{1,0:T(8,128)S(1)} collective-permute-done((f32[16,384]{1,0:T(8,128)S(1)}, f32[16,384]{1,0:T(8,128)S(1)}, u32[]{:S(2)}, u32[]{:S(2)}) %collective-permute-start.1) | collective-permute-done | bytes 24608 | tf_op jit(solution)/shard_map/ppermute | solution.py:39
  15.2 1.8 %collective-permute-start.2 = (f32[16,384]{1,0:T(8,128)S(1)}, f32[16,384]{1,0:T(8,128)S(1)}, u32[]{:S(2)}, u32[]{:S(2)}) collective-permute-start(f32[16,384]{1,0:T(8,128)S(1)} %add.16), channel_id=1, source_target_pairs={{0,4},{2,6},{4,0},{6,2},{8,12},{10,14},{12,8},{14,10},{16,20},{18,... | collective-permute-start | bytes 73736 | tf_op jit(solution)/shard_map/ppermute | solution.py:39
  17.0 2.1 %collective-permute-done.2 = f32[16,384]{1,0:T(8,128)S(1)} collective-permute-done((f32[16,384]{1,0:T(8,128)S(1)}, f32[16,384]{1,0:T(8,128)S(1)}, u32[]{:S(2)}, u32[]{:S(2)}) %collective-permute-start.2) | collective-permute-done | bytes 24608 | tf_op jit(solution)/shard_map/ppermute | solution.py:39
  19.1 1.8 %collective-permute-start.3 = (f32[16,384]{1,0:T(8,128)S(1)}, f32[16,384]{1,0:T(8,128)S(1)}, u32[]{:S(2)}, u32[]{:S(2)}) collective-permute-start(f32[16,384]{1,0:T(8,128)S(1)} %add.17), channel_id=1, source_target_pairs={{0,8},{2,10},{4,12},{6,14},{8,0},{10,2},{12,4},{14,6},{16,24},{18,... | collective-permute-start | bytes 73736 | tf_op jit(solution)/shard_map/ppermute | solution.py:39
  20.9 2.0 %collective-permute-done.3 = f32[16,384]{1,0:T(8,128)S(1)} collective-permute-done((f32[16,384]{1,0:T(8,128)S(1)}, f32[16,384]{1,0:T(8,128)S(1)}, u32[]{:S(2)}, u32[]{:S(2)}) %collective-permute-start.3) | collective-permute-done | bytes 24608 | tf_op jit(solution)/shard_map/ppermute | solution.py:39
  22.9 2.8 %collective-permute-start.4 = (f32[16,384]{1,0:T(8,128)S(1)}, f32[16,384]{1,0:T(8,128)S(1)}, u32[]{:S(2)}, u32[]{:S(2)}) collective-permute-start(f32[16,384]{1,0:T(8,128)S(1)} %add.18), channel_id=1, source_target_pairs={{0,16},{2,18},{4,20},{6,22},{8,24},{10,26},{12,28},{14,30},{16,0},... | collective-permute-start | bytes 73736 | tf_op jit(solution)/shard_map/ppermute | solution.py:39
  25.8 1.9 %collective-permute-done.4 = f32[16,384]{1,0:T(8,128)S(1)} collective-permute-done((f32[16,384]{1,0:T(8,128)S(1)}, f32[16,384]{1,0:T(8,128)S(1)}, u32[]{:S(2)}, u32[]{:S(2)}) %collective-permute-start.4) | collective-permute-done | bytes 24608 | tf_op jit(solution)/shard_map/ppermute | solution.py:39
  27.7 0.3 center.1
  28.0 1.8 %collective-permute-start.14 = (bf16[16,16,512]{2,1,0:T(8,128)(2,1)S(1)}, bf16[16,16,512]{2,1,0:T(8,128)(2,1)S(1)}, u32[]{:S(2)}, u32[]{:S(2)}) collective-permute-start(bf16[16,16,512]{2,1,0:T(8,128)(2,1)S(1)} %center.1), channel_id=1, source_target_pairs={{0,1},{1,0},{2,3},{3,2},{4,5},{5,4},{6,7},{7,6},{8,9},{9,8},{10,11... | collective-permute-start | bytes 786440 | tf_op jit(solution)/shard_map/ppermute | solution.py:403
  29.8 2.5 %stage.1.expression_ref = bf16[512,5120]{1,0:T(8,128)(2,1)S(1)} custom-call(bf16[512,5120]{1,0:T(8,128)(2,1)} %source_ref.1), custom_call_target="tpu_custom_call" | custom-call | tf_op jit(solution)/shard_map/stage/pallas_call | solution.py:228
  32.3 2.1 %collective-permute-done.14 = bf16[16,16,512]{2,1,0:T(8,128)(2,1)S(1)} collective-permute-done((bf16[16,16,512]{2,1,0:T(8,128)(2,1)S(1)}, bf16[16,16,512]{2,1,0:T(8,128)(2,1)S(1)}, u32[]{:S(2)}, u32[]{:S(2)}) %collective-permute-start.14) | collective-permute-done | bytes 262176 | tf_op jit(solution)/shard_map/ppermute | solution.py:403
  34.4 1.5 %shard_map.67 = (bf16[128,3072]{1,0:T(8,128)(2,1)S(1)}, f32[128,3072]{1,0:T(8,128)S(1)}) custom-call(s32[2]{0:T(128)S(1)} %pad_add_fusion.where_ref, bf16[8,2,16,512]{3,2,1,0:T(8,128)(2,1)S(1)} %bitcast.44, bf16[512,5120]{1,0:T(8,128)(2,1)S(1)} %stage.1.expression_ref), custom_call_target="tpu_custom_call" | custom-call | tf_op jit(solution)/shard_map/pallas_call | solution.py:268
  36.0 1.5 %shard_map.55 = (bf16[128,2944]{1,0:T(8,128)(2,1)S(1)}, f32[128,2944]{1,0:T(8,128)S(1)}) custom-call(s32[2]{0:T(128)S(1)} %pad_add_fusion.where_ref, bf16[8,2,16,512]{3,2,1,0:T(8,128)(2,1)S(1)} %bitcast.38, bf16[512,5120]{1,0:T(8,128)(2,1)S(1)} %stage.1.expression_ref), custom_call_target="tpu_custom_call" | custom-call | tf_op jit(solution)/shard_map/pallas_call | solution.py:268
  37.5 0.6 collective-permute-start.6
  38.1 1.3 %shard_map.59 = (bf16[128,2304]{1,0:T(8,128)(2,1)S(1)}, f32[128,2304]{1,0:T(8,128)S(1)}) custom-call(s32[2]{0:T(128)S(1)} %pad_add_fusion.where_ref, bf16[8,2,16,512]{3,2,1,0:T(8,128)(2,1)S(1)} %bitcast.39, bf16[512,5120]{1,0:T(8,128)(2,1)S(1)} %stage.1.expression_ref), custom_call_target="tpu_custom_call" | custom-call | tf_op jit(solution)/shard_map/pallas_call | solution.py:268
  39.5 1.3 %shard_map.63 = (bf16[128,2176]{1,0:T(8,128)(2,1)S(1)}, f32[128,2176]{1,0:T(8,128)S(1)}) custom-call(s32[2]{0:T(128)S(1)} %pad_add_fusion.where_ref, bf16[8,2,16,512]{3,2,1,0:T(8,128)(2,1)S(1)} %bitcast.45, bf16[512,5120]{1,0:T(8,128)(2,1)S(1)} %stage.1.expression_ref), custom_call_target="tpu_custom_call" | custom-call | tf_op jit(solution)/shard_map/pallas_call | solution.py:268
  40.7 0.6 collective-permute-start.15
  41.3 0.7 shard_map.68
  42.0 1.9 %collective-permute-start.20 = (bf16[2,32,3072]{2,1,0:T(8,128)(2,1)S(1)}, bf16[2,32,3072]{2,1,0:T(8,128)(2,1)S(1)}, u32[]{:S(2)}, u32[]{:S(2)}) collective-permute-start(bf16[2,32,3072]{2,1,0:T(8,128)(2,1)S(1)} %get-tuple-element.72), channel_id=1, source_target_pairs={{0,8},{2,10},{4,12},{6,14},{8,0},{10,2},{12,4},{14,6},{16,24},{18,... | collective-permute-start | bytes 1179656 | tf_op jit(solution)/shard_map/ppermute | solution.py:325
  43.9 0.7 shard_map.56
  44.6 1.6 %collective-permute-start.7 = (bf16[4,16,2944]{2,1,0:T(8,128)(2,1)S(1)}, bf16[4,16,2944]{2,1,0:T(8,128)(2,1)S(1)}, u32[]{:S(2)}, u32[]{:S(2)}) collective-permute-start(bf16[4,16,2944]{2,1,0:T(8,128)(2,1)S(1)} %get-tuple-element.48), channel_id=1, source_target_pairs={{0,4},{2,6},{4,0},{6,2},{8,12},{10,14},{12,8},{14,10},{16,20},{18,... | collective-permute-start | bytes 1130504 | tf_op jit(solution)/shard_map/ppermute | solution.py:325
  46.2 0.7 shard_map.60
  46.8 0.6 collective-permute-start.11
  47.4 0.7 shard_map.64
  48.0 1.6 %collective-permute-start.16 = (bf16[4,16,2176]{2,1,0:T(8,128)(2,1)S(1)}, bf16[4,16,2176]{2,1,0:T(8,128)(2,1)S(1)}, u32[]{:S(2)}, u32[]{:S(2)}) collective-permute-start(bf16[4,16,2176]{2,1,0:T(8,128)(2,1)S(1)} %get-tuple-element.64), channel_id=1, source_target_pairs={{0,4},{2,6},{4,0},{6,2},{8,12},{10,14},{12,8},{14,10},{16,20},{18,... | collective-permute-start | bytes 835592 | tf_op jit(solution)/shard_map/ppermute | solution.py:325
  49.6 3.5 %collective-permute-done.20 = bf16[2,32,3072]{2,1,0:T(8,128)(2,1)S(1)} collective-permute-done((bf16[2,32,3072]{2,1,0:T(8,128)(2,1)S(1)}, bf16[2,32,3072]{2,1,0:T(8,128)(2,1)S(1)}, u32[]{:S(2)}, u32[]{:S(2)}) %collective-permute-start.20) | collective-permute-done | bytes 393248 | tf_op jit(solution)/shard_map/ppermute | solution.py:325
  53.2 0.6 shard_map.69
  53.8 1.7 %collective-permute-start.21 = (bf16[2,16,3072]{2,1,0:T(8,128)(2,1)S(1)}, bf16[2,16,3072]{2,1,0:T(8,128)(2,1)S(1)}, u32[]{:S(2)}, u32[]{:S(2)}) collective-permute-start(bf16[2,16,3072]{2,1,0:T(8,128)(2,1)S(1)} %get-tuple-element.74), channel_id=1, source_target_pairs={{0,4},{2,6},{4,0},{6,2},{8,12},{10,14},{12,8},{14,10},{16,20},{18,... | collective-permute-start | bytes 589832 | tf_op jit(solution)/shard_map/ppermute | solution.py:325
  55.5 0.7 collective-permute-done.7
  56.3 0.6 shard_map.57
  56.9 0.9 %collective-permute-start.8 = (bf16[2,16,2944]{2,1,0:T(8,128)(2,1)S(1)}, bf16[2,16,2944]{2,1,0:T(8,128)(2,1)S(1)}, u32[]{:S(2)}, u32[]{:S(2)}) collective-permute-start(bf16[2,16,2944]{2,1,0:T(8,128)(2,1)S(1)} %get-tuple-element.50), channel_id=1, source_target_pairs={{0,8},{2,10},{4,12},{6,14},{8,0},{10,2},{12,4},{14,6},{16,24},{18,... | collective-permute-start | bytes 565256 | tf_op jit(solution)/shard_map/ppermute | solution.py:325
  57.8 4.8 %collective-permute-done.11 = bf16[4,16,2304]{2,1,0:T(8,128)(2,1)S(1)} collective-permute-done((bf16[4,16,2304]{2,1,0:T(8,128)(2,1)S(1)}, bf16[4,16,2304]{2,1,0:T(8,128)(2,1)S(1)}, u32[]{:S(2)}, u32[]{:S(2)}) %collective-permute-start.11) | collective-permute-done | bytes 294944 | tf_op jit(solution)/shard_map/ppermute | solution.py:325
  62.6 0.6 shard_map.61
  63.4 5.1 %collective-permute-done.16 = bf16[4,16,2176]{2,1,0:T(8,128)(2,1)S(1)} collective-permute-done((bf16[4,16,2176]{2,1,0:T(8,128)(2,1)S(1)}, bf16[4,16,2176]{2,1,0:T(8,128)(2,1)S(1)}, u32[]{:S(2)}, u32[]{:S(2)}) %collective-permute-start.16) | collective-permute-done | bytes 278560 | tf_op jit(solution)/shard_map/ppermute | solution.py:325
  68.5 0.6 shard_map.65
  69.4 2.1 %collective-permute-done.21 = bf16[2,16,3072]{2,1,0:T(8,128)(2,1)S(1)} collective-permute-done((bf16[2,16,3072]{2,1,0:T(8,128)(2,1)S(1)}, bf16[2,16,3072]{2,1,0:T(8,128)(2,1)S(1)}, u32[]{:S(2)}, u32[]{:S(2)}) %collective-permute-start.21) | collective-permute-done | bytes 196640 | tf_op jit(solution)/shard_map/ppermute | solution.py:325
  71.5 0.6 shard_map.70
  72.1 2.8 %collective-permute-start.22 = (bf16[1,16,3072]{2,1,0:T(8,128)(2,1)S(1)}, bf16[1,16,3072]{2,1,0:T(8,128)(2,1)S(1)}, u32[]{:S(2)}, u32[]{:S(2)}) collective-permute-start(bf16[1,16,3072]{2,1,0:T(8,128)(2,1)S(1)} %get-tuple-element.76), channel_id=1, source_target_pairs={{0,16},{2,18},{4,20},{6,22},{8,24},{10,26},{12,28},{14,30},{16,0},... | collective-permute-start | bytes 294920 | tf_op jit(solution)/shard_map/ppermute | solution.py:325
  74.9 0.6 shard_map.58
  75.8 0.6 shard_map.62
  76.4 2.8 %collective-permute-start.13 = (bf16[1,16,2304]{2,1,0:T(8,128)(2,1)S(1)}, bf16[1,16,2304]{2,1,0:T(8,128)(2,1)S(1)}, u32[]{:S(2)}, u32[]{:S(2)}) collective-permute-start(bf16[1,16,2304]{2,1,0:T(8,128)(2,1)S(1)} %get-tuple-element.60), channel_id=1, source_target_pairs={{0,16},{2,18},{4,20},{6,22},{8,24},{10,26},{12,28},{14,30},{16,0},... | collective-permute-start | bytes 221192 | tf_op jit(solution)/shard_map/ppermute | solution.py:325
  79.2 0.6 shard_map.66
  80.0 8.1 %collective-permute-done.13 = bf16[1,16,2304]{2,1,0:T(8,128)(2,1)S(1)} collective-permute-done((bf16[1,16,2304]{2,1,0:T(8,128)(2,1)S(1)}, bf16[1,16,2304]{2,1,0:T(8,128)(2,1)S(1)}, u32[]{:S(2)}, u32[]{:S(2)}) %collective-permute-start.13) | collective-permute-done | bytes 73760 | tf_op jit(solution)/shard_map/ppermute | solution.py:325
  88.1 0.8 collective-permute-done.18
  88.9 1.6 %finish.1 = f32[2,16,5120]{2,1,0:T(8,128)} custom-call(s32[2]{0:T(128)S(1)} %pad_add_fusion.where_ref, f32[16,2944]{1,0:T(8,128)S(1)} %bitcast.65, bf16[16,2944]{1,0:T(8,128)(2,1)S(1)} %bitcast.71, f32[16,2304]{1,0:T(8,128)S(1)} %bitcast.66, bf16[16,2304]{1,0:T(8,128)(2,1)S(1)} %bitcast.72, f32[16,2176]{1,0:T(8,128)S(1)} %bitcast.68, ...), custom_call_target="tpu_custom_call" | custom-call | tf_op jit(solution)/shard_map/finish/pallas_call | solution.py:355
  (26 shorter events, 1.4 us)
Async XLA Ops:
  0.1 27.6 %copy-start = (s32[512,1]{0,1:T(1,128)S(1)}, s32[512,1]{0,1:T(1,128)}, u32[]{:S(2)}) copy-start(s32[512,1]{0,1:T(1,128)} %param.8) | copy-start | bytes 6148
  4.2 23.5 %collective-permute-start.5 = (bf16[16,16,512]{2,1,0:T(8,128)(2,1)S(1)}, bf16[16,16,512]{2,1,0:T(8,128)(2,1)S(1)}, u32[]{:S(2)}, u32[]{:S(2)}) collective-permute-start(bf16[16,16,512]{2,1,0:T(8,128)(2,1)S(1)} %get-tuple-element.44), channel_id=1, source_target_pairs={{0,1},{1,0},{2,3},{3,2},{4,5},{5,4},{6,7},{7,6},{8,9},{9,8},{10,11... | collective-permute-start | bytes 786440 | tf_op jit(solution)/shard_map/ppermute | solution.py:396
  7.2 6.8 %collective-permute-start = (f32[16,384]{1,0:T(8,128)S(1)}, f32[16,384]{1,0:T(8,128)S(1)}, u32[]{:S(2)}, u32[]{:S(2)}) collective-permute-start(f32[16,384]{1,0:T(8,128)S(1)} %get-tuple-element.43), channel_id=1, source_target_pairs={{0,1},{1,0},{2,3},{3,2},{4,5},{5,4},{6,7},{7,6},{8,9},{9,8},{10,11... | collective-permute-start | bytes 73736 | tf_op jit(solution)/shard_map/ppermute | solution.py:395
  14.0 1.2 %collective-permute-start.1 = (f32[16,384]{1,0:T(8,128)S(1)}, f32[16,384]{1,0:T(8,128)S(1)}, u32[]{:S(2)}, u32[]{:S(2)}) collective-permute-start(f32[16,384]{1,0:T(8,128)S(1)} %add.15), channel_id=1, source_target_pairs={{0,2},{2,0},{4,6},{6,4},{8,10},{10,8},{12,14},{14,12},{16,18},{18,... | collective-permute-start | bytes 73736 | tf_op jit(solution)/shard_map/ppermute | solution.py:39
  15.2 3.8 %collective-permute-start.2 = (f32[16,384]{1,0:T(8,128)S(1)}, f32[16,384]{1,0:T(8,128)S(1)}, u32[]{:S(2)}, u32[]{:S(2)}) collective-permute-start(f32[16,384]{1,0:T(8,128)S(1)} %add.16), channel_id=1, source_target_pairs={{0,4},{2,6},{4,0},{6,2},{8,12},{10,14},{12,8},{14,10},{16,20},{18,... | collective-permute-start | bytes 73736 | tf_op jit(solution)/shard_map/ppermute | solution.py:39
  19.1 3.8 %collective-permute-start.3 = (f32[16,384]{1,0:T(8,128)S(1)}, f32[16,384]{1,0:T(8,128)S(1)}, u32[]{:S(2)}, u32[]{:S(2)}) collective-permute-start(f32[16,384]{1,0:T(8,128)S(1)} %add.17), channel_id=1, source_target_pairs={{0,8},{2,10},{4,12},{6,14},{8,0},{10,2},{12,4},{14,6},{16,24},{18,... | collective-permute-start | bytes 73736 | tf_op jit(solution)/shard_map/ppermute | solution.py:39
  22.9 4.7 %collective-permute-start.4 = (f32[16,384]{1,0:T(8,128)S(1)}, f32[16,384]{1,0:T(8,128)S(1)}, u32[]{:S(2)}, u32[]{:S(2)}) collective-permute-start(f32[16,384]{1,0:T(8,128)S(1)} %add.18), channel_id=1, source_target_pairs={{0,16},{2,18},{4,20},{6,22},{8,24},{10,26},{12,28},{14,30},{16,0},... | collective-permute-start | bytes 73736 | tf_op jit(solution)/shard_map/ppermute | solution.py:39
  28.0 6.4 %collective-permute-start.14 = (bf16[16,16,512]{2,1,0:T(8,128)(2,1)S(1)}, bf16[16,16,512]{2,1,0:T(8,128)(2,1)S(1)}, u32[]{:S(2)}, u32[]{:S(2)}) collective-permute-start(bf16[16,16,512]{2,1,0:T(8,128)(2,1)S(1)} %center.1), channel_id=1, source_target_pairs={{0,1},{1,0},{2,3},{3,2},{4,5},{5,4},{6,7},{7,6},{8,9},{9,8},{10,11... | collective-permute-start | bytes 786440 | tf_op jit(solution)/shard_map/ppermute | solution.py:403
  36.0 5.3 %collective-permute-start.19 = (bf16[128,3072]{1,0:T(8,128)(2,1)S(1)}, bf16[128,3072]{1,0:T(8,128)(2,1)S(1)}, u32[]{:S(2)}, u32[]{:S(2)}) collective-permute-start(bf16[128,3072]{1,0:T(8,128)(2,1)S(1)} %get-tuple-element.70), channel_id=1, source_target_pairs={{0,2},{2,0},{4,6},{6,4},{8,10},{10,8},{12,14},{14,12},{16,18},{18,... | collective-permute-start | bytes 2359304 | tf_op jit(solution)/shard_map/ppermute | solution.py:325
  37.5 6.4 %collective-permute-start.6 = (bf16[128,2944]{1,0:T(8,128)(2,1)S(1)}, bf16[128,2944]{1,0:T(8,128)(2,1)S(1)}, u32[]{:S(2)}, u32[]{:S(2)}) collective-permute-start(bf16[128,2944]{1,0:T(8,128)(2,1)S(1)} %get-tuple-element.46), channel_id=1, source_target_pairs={{0,2},{2,0},{4,6},{6,4},{8,10},{10,8},{12,14},{14,12},{16,18},{18,... | collective-permute-start | bytes 2261000 | tf_op jit(solution)/shard_map/ppermute | solution.py:325
  39.4 6.8 %collective-permute-start.10 = (bf16[128,2304]{1,0:T(8,128)(2,1)S(1)}, bf16[128,2304]{1,0:T(8,128)(2,1)S(1)}, u32[]{:S(2)}, u32[]{:S(2)}) collective-permute-start(bf16[128,2304]{1,0:T(8,128)(2,1)S(1)} %get-tuple-element.54), channel_id=1, source_target_pairs={{0,2},{2,0},{4,6},{6,4},{8,10},{10,8},{12,14},{14,12},{16,18},{18,... | collective-permute-start | bytes 1769480 | tf_op jit(solution)/shard_map/ppermute | solution.py:325
  40.7 6.6 %collective-permute-start.15 = (bf16[128,2176]{1,0:T(8,128)(2,1)S(1)}, bf16[128,2176]{1,0:T(8,128)(2,1)S(1)}, u32[]{:S(2)}, u32[]{:S(2)}) collective-permute-start(bf16[128,2176]{1,0:T(8,128)(2,1)S(1)} %get-tuple-element.62), channel_id=1, source_target_pairs={{0,2},{2,0},{4,6},{6,4},{8,10},{10,8},{12,14},{14,12},{16,18},{18,... | collective-permute-start | bytes 1671176 | tf_op jit(solution)/shard_map/ppermute | solution.py:325
  42.0 11.2 %collective-permute-start.20 = (bf16[2,32,3072]{2,1,0:T(8,128)(2,1)S(1)}, bf16[2,32,3072]{2,1,0:T(8,128)(2,1)S(1)}, u32[]{:S(2)}, u32[]{:S(2)}) collective-permute-start(bf16[2,32,3072]{2,1,0:T(8,128)(2,1)S(1)} %get-tuple-element.72), channel_id=1, source_target_pairs={{0,8},{2,10},{4,12},{6,14},{8,0},{10,2},{12,4},{14,6},{16,24},{18,... | collective-permute-start | bytes 1179656 | tf_op jit(solution)/shard_map/ppermute | solution.py:325
  44.6 11.7 %collective-permute-start.7 = (bf16[4,16,2944]{2,1,0:T(8,128)(2,1)S(1)}, bf16[4,16,2944]{2,1,0:T(8,128)(2,1)S(1)}, u32[]{:S(2)}, u32[]{:S(2)}) collective-permute-start(bf16[4,16,2944]{2,1,0:T(8,128)(2,1)S(1)} %get-tuple-element.48), channel_id=1, source_target_pairs={{0,4},{2,6},{4,0},{6,2},{8,12},{10,14},{12,8},{14,10},{16,20},{18,... | collective-permute-start | bytes 1130504 | tf_op jit(solution)/shard_map/ppermute | solution.py:325
  46.8 15.8 %collective-permute-start.11 = (bf16[4,16,2304]{2,1,0:T(8,128)(2,1)S(1)}, bf16[4,16,2304]{2,1,0:T(8,128)(2,1)S(1)}, u32[]{:S(2)}, u32[]{:S(2)}) collective-permute-start(bf16[4,16,2304]{2,1,0:T(8,128)(2,1)S(1)} %get-tuple-element.56), channel_id=1, source_target_pairs={{0,4},{2,6},{4,0},{6,2},{8,12},{10,14},{12,8},{14,10},{16,20},{18,... | collective-permute-start | bytes 884744 | tf_op jit(solution)/shard_map/ppermute | solution.py:325
  48.0 20.5 %collective-permute-start.16 = (bf16[4,16,2176]{2,1,0:T(8,128)(2,1)S(1)}, bf16[4,16,2176]{2,1,0:T(8,128)(2,1)S(1)}, u32[]{:S(2)}, u32[]{:S(2)}) collective-permute-start(bf16[4,16,2176]{2,1,0:T(8,128)(2,1)S(1)} %get-tuple-element.64), channel_id=1, source_target_pairs={{0,4},{2,6},{4,0},{6,2},{8,12},{10,14},{12,8},{14,10},{16,20},{18,... | collective-permute-start | bytes 835592 | tf_op jit(solution)/shard_map/ppermute | solution.py:325
  53.8 17.8 %collective-permute-start.21 = (bf16[2,16,3072]{2,1,0:T(8,128)(2,1)S(1)}, bf16[2,16,3072]{2,1,0:T(8,128)(2,1)S(1)}, u32[]{:S(2)}, u32[]{:S(2)}) collective-permute-start(bf16[2,16,3072]{2,1,0:T(8,128)(2,1)S(1)} %get-tuple-element.74), channel_id=1, source_target_pairs={{0,4},{2,6},{4,0},{6,2},{8,12},{10,14},{12,8},{14,10},{16,20},{18,... | collective-permute-start | bytes 589832 | tf_op jit(solution)/shard_map/ppermute | solution.py:325
  56.9 18.0 %collective-permute-start.8 = (bf16[2,16,2944]{2,1,0:T(8,128)(2,1)S(1)}, bf16[2,16,2944]{2,1,0:T(8,128)(2,1)S(1)}, u32[]{:S(2)}, u32[]{:S(2)}) collective-permute-start(bf16[2,16,2944]{2,1,0:T(8,128)(2,1)S(1)} %get-tuple-element.50), channel_id=1, source_target_pairs={{0,8},{2,10},{4,12},{6,14},{8,0},{10,2},{12,4},{14,6},{16,24},{18,... | collective-permute-start | bytes 565256 | tf_op jit(solution)/shard_map/ppermute | solution.py:325
  63.2 12.6 %collective-permute-start.12 = (bf16[2,16,2304]{2,1,0:T(8,128)(2,1)S(1)}, bf16[2,16,2304]{2,1,0:T(8,128)(2,1)S(1)}, u32[]{:S(2)}, u32[]{:S(2)}) collective-permute-start(bf16[2,16,2304]{2,1,0:T(8,128)(2,1)S(1)} %get-tuple-element.58), channel_id=1, source_target_pairs={{0,8},{2,10},{4,12},{6,14},{8,0},{10,2},{12,4},{14,6},{16,24},{18,... | collective-permute-start | bytes 442376 | tf_op jit(solution)/shard_map/ppermute | solution.py:325
  69.2 10.0 %collective-permute-start.17 = (bf16[2,16,2176]{2,1,0:T(8,128)(2,1)S(1)}, bf16[2,16,2176]{2,1,0:T(8,128)(2,1)S(1)}, u32[]{:S(2)}, u32[]{:S(2)}) collective-permute-start(bf16[2,16,2176]{2,1,0:T(8,128)(2,1)S(1)} %get-tuple-element.66), channel_id=1, source_target_pairs={{0,8},{2,10},{4,12},{6,14},{8,0},{10,2},{12,4},{14,6},{16,24},{18,... | collective-permute-start | bytes 417800 | tf_op jit(solution)/shard_map/ppermute | solution.py:325
  72.1 16.8 %collective-permute-start.22 = (bf16[1,16,3072]{2,1,0:T(8,128)(2,1)S(1)}, bf16[1,16,3072]{2,1,0:T(8,128)(2,1)S(1)}, u32[]{:S(2)}, u32[]{:S(2)}) collective-permute-start(bf16[1,16,3072]{2,1,0:T(8,128)(2,1)S(1)} %get-tuple-element.76), channel_id=1, source_target_pairs={{0,16},{2,18},{4,20},{6,22},{8,24},{10,26},{12,28},{14,30},{16,0},... | collective-permute-start | bytes 294920 | tf_op jit(solution)/shard_map/ppermute | solution.py:325
  75.5 13.4 %collective-permute-start.9 = (bf16[1,16,2944]{2,1,0:T(8,128)(2,1)S(1)}, bf16[1,16,2944]{2,1,0:T(8,128)(2,1)S(1)}, u32[]{:S(2)}, u32[]{:S(2)}) collective-permute-start(bf16[1,16,2944]{2,1,0:T(8,128)(2,1)S(1)} %get-tuple-element.52), channel_id=1, source_target_pairs={{0,16},{2,18},{4,20},{6,22},{8,24},{10,26},{12,28},{14,30},{16,0},... | collective-permute-start | bytes 282632 | tf_op jit(solution)/shard_map/ppermute | solution.py:325
  76.4 11.7 %collective-permute-start.13 = (bf16[1,16,2304]{2,1,0:T(8,128)(2,1)S(1)}, bf16[1,16,2304]{2,1,0:T(8,128)(2,1)S(1)}, u32[]{:S(2)}, u32[]{:S(2)}) collective-permute-start(bf16[1,16,2304]{2,1,0:T(8,128)(2,1)S(1)} %get-tuple-element.60), channel_id=1, source_target_pairs={{0,16},{2,18},{4,20},{6,22},{8,24},{10,26},{12,28},{14,30},{16,0},... | collective-permute-start | bytes 221192 | tf_op jit(solution)/shard_map/ppermute | solution.py:325
  79.7 9.2 %collective-permute-start.18 = (bf16[1,16,2176]{2,1,0:T(8,128)(2,1)S(1)}, bf16[1,16,2176]{2,1,0:T(8,128)(2,1)S(1)}, u32[]{:S(2)}, u32[]{:S(2)}) collective-permute-start(bf16[1,16,2176]{2,1,0:T(8,128)(2,1)S(1)} %get-tuple-element.68), channel_id=1, source_target_pairs={{0,16},{2,18},{4,20},{6,22},{8,24},{10,26},{12,28},{14,30},{16,0},... | collective-permute-start | bytes 208904 | tf_op jit(solution)/shard_map/ppermute | solution.py:325
